TPU v7x, 128 devices: a whole 4x4x4 slice. The times are simulated.
128 devices in a mesh: grp: 16 (over z, x_lo, core), blk: 8 (over x_hi, y).
Axes of the slice: x: 4 (x_hi: 2, x_lo: 2; x = x_hi * 2 + x_lo), y: 4, z: 4, core: 2. Of those that a mesh axis runs over, the one named last changes fastest.
Arguments:
- temp: float32 [8, 1024, 1024], P(None, 'grp', 'blk'), may hold values from -6 to 6
- uvel: float32 [8, 1024, 1024], P(None, 'grp', 'blk'), may hold values from -0.4 to 0.4
- vvel: float32 [8, 1024, 1024], P(None, 'grp', 'blk'), may hold values from -0.4 to 0.4
- couple_col: int32 [16, 8, 2048], P('grp', 'blk'), may hold values from 0 to 8191
- couple_cell: int32 [16, 8, 2048], P('grp', 'blk'), may hold values from 0 to 1048575
- cavity: int32 [16, 8, 2048], P('grp', 'blk'), may hold values 0 or 1
- thickness: float32 [1024, 1024], P('blk'), may hold values from 0.2 to 2
- viscosity: float32 [1024, 1024], P('blk'), may hold values from 0.5 to 4
- friction: float32 [1024, 1024], P('blk'), may hold values from 0.02 to 0.3
- drive: float32 [1024, 1024], P('blk'), may hold values from -6 to 6
Outputs:
- temp_new: float32 [8, 1024, 1024], P(None, 'grp', 'blk')
- ice_velocity: float32 [1024, 1024], P('blk')
Inputs may be any that keep to these rules, and one draw needn't show every extreme that they name: `couple_col`: an index of a column within the 64 x 128 block of the device holding the entry, row-major. `couple_cell`: a row-major index into the whole ice grid.
All inputs are finite; a program needn't handle non-finite values. No bound on the sum of `cavity` on one device may be relied on, other than what follows from the above.
Results may differ from a plain program's by a relative error of at most 0.0003.
Values sent between devices are 32-bit elements; how exact they have to be, the bound alone decides.
No kernel may reach another device: no remote copies, remote signals or barrier semaphores. Data moves between devices by JAX's collectives and lax.ppermute only.
A program may use at most 64 MiB of HBM per device.

v0:
```python
import functools
import jax
import jax.numpy as jnp
from jax import lax
from jax.experimental import pallas as pl
from jax.experimental.pallas import tpu as pltpu
from jax.sharding import Mesh
from jax.sharding import PartitionSpec as P


LEVELS = 3
CYCLES = 2
GRP = ("z", "xl", "co")
ZX = ("z", "xl")
BLK = ("xh", "y")
omega = 0.8
kappa = 0.1
vertical_mix = 0.2
melt_rate = 0.5

LEV = 8
CX = 64
CY = 128
ROWS = 128
COLS = 1024
HALF = 64
ENT = 2048
EXT = 192
KC = 512
CELLS = ROWS * COLS
f32 = jnp.float32
bf16 = jnp.bfloat16
i32 = jnp.int32
VMEM = pl.BlockSpec(memory_space=pltpu.VMEM)
SMEM = pl.BlockSpec(memory_space=pltpu.SMEM)


def cost(us):
    return pl.CostEstimate(flops=int(us * 2e7), bytes_accessed=0, transcendentals=0)


def split2(x):
    high = x.astype(bf16)
    low = (x - high.astype(f32)).astype(bf16)
    return high, low


def split3(x):
    high = x.astype(bf16)
    rest = x - high.astype(f32)
    mid = rest.astype(bf16)
    return high, mid, (rest - mid.astype(f32)).astype(bf16)


def sub_iota(shape):
    return lax.broadcasted_iota(i32, shape, 0)


def lane_iota(shape):
    return lax.broadcasted_iota(i32, shape, 1)


NT = (((1,), (1,)), ((), ()))


def pack_kernel(where, temp, uvel, vvel, col, cell, cav, packet, row_a, row_b, col_a, col_b):
    even_row, even_col = where[1] == 0, where[3] == 0
    tops = split3(temp[0].T)
    table = jnp.concatenate(tops, axis=0)
    for j in range(ENT // KC):
        c = col[0, :, j * KC : (j + 1) * KC]
        rows = jnp.where(sub_iota((CX, KC)) == (c >> 7), 1.0, 0.0).astype(bf16)
        picked = jnp.dot(table, rows, preferred_element_type=f32)
        picked = picked[0:128] + picked[128:256] + picked[256:384]
        mask = sub_iota((CY, KC)) == (c & 127)
        top = jnp.sum(jnp.where(mask, picked, 0.0), axis=0, keepdims=True)
        on = cav[0, :, j * KC : (j + 1) * KC] > 0
        index = jnp.where(on, cell[0, :, j * KC : (j + 1) * KC], -1)
        packet[0:1, j * KC : (j + 1) * KC] = index.astype(f32)
        packet[1:2, j * KC : (j + 1) * KC] = top
    for k in range(LEV):
        for field, at in ((temp, k), (uvel, k + 8)):
            low, high = field[k, 0:1, :], field[k, CX - 1 : CX, :]
            row_a[at : at + 1, :] = jnp.where(even_row, high, low)
            row_b[at : at + 1, :] = jnp.where(even_row, low, high)
        for field, at in ((temp, k), (vvel, k + 8)):
            across = field[k].T
            low, high = across[0:1, :], across[CY - 1 : CY, :]
            col_a[at : at + 1, :] = jnp.where(even_col, high, low)
            col_b[at : at + 1, :] = jnp.where(even_col, low, high)


def pack(where, temp, uvel, vvel, col, cell, cav):
    return pl.pallas_call(
        pack_kernel,
        out_shape=(
            jax.ShapeDtypeStruct((2, ENT), f32),
            jax.ShapeDtypeStruct((16, CY), f32),
            jax.ShapeDtypeStruct((16, CY), f32),
            jax.ShapeDtypeStruct((16, CX), f32),
            jax.ShapeDtypeStruct((16, CX), f32),
        ),
        in_specs=[SMEM] + [VMEM] * 6,
        out_specs=(VMEM,) * 5,
        cost_estimate=cost(3),
        name="pack",
    )(where, temp, uvel, vvel, col, cell, cav)


def place(packets, first, k):
    at = pl.multiple_of((k % (ENT // KC)) * KC, KC)
    index = packets[k // (ENT // KC), 0:1, pl.ds(at, KC)].astype(i32)
    local = index - first
    row = local >> 10
    spot = ((row >> 3) << 6) | (((local >> 7) & 7) << 3) | (row & 7)
    spot = jnp.where((local >= 0) & (local < CELLS), spot, -1)
    return spot, local & 127, at


def couple_kernel(where, packets, thick, mine, other, near, far, tiles, table, onehot, lanes, acc, melt):
    first, core = where[0], where[1]
    acc[...] = jnp.zeros_like(acc)
    for t in range(128):
        i, c = t // 8, t % 8
        tiles[t * 8 : t * 8 + 8, :] = thick[i * 8 : i * 8 + 8, c * 128 : c * 128 + 128]
    for a in range(8):
        high, low = split2(tiles[a * 128 : a * 128 + 128, :].T)
        table[0:128, a * 128 : a * 128 + 128] = high
        table[128:256, a * 128 : a * 128 + 128] = low

    def fetch(k, p, out):
        spot, lane, at = place(packets, first, k)
        onehot[p] = jnp.where(lax.broadcasted_iota(jnp.int16, (1024, KC), 0) == spot.astype(jnp.int16), jnp.array(1.0, bf16), jnp.array(0.0, bf16))
        picked = jnp.dot(table[...], onehot[p], preferred_element_type=f32)
        picked = picked[0:128] + picked[128:256]
        mask = sub_iota((128, KC)) == lane
        draft = jnp.sum(jnp.where(mask, picked, 0.0), axis=0, keepdims=True)
        s = k // (ENT // KC)
        out[s % 4, 0:1, pl.ds(at, KC)] = draft
        value = melt_rate * (packets[s, 1:2, pl.ds(at, KC)] + 0.5 + 0.5 * draft)
        high, low = split2(value)
        mask = lax.broadcasted_iota(jnp.int16, (128, KC), 0) == lane.astype(jnp.int16)
        zero = jnp.array(0.0, bf16)
        lanes[p, 0:128, :] = jnp.where(mask, high, zero)
        lanes[p, 128:256, :] = jnp.where(mask, low, zero)

    def spread(p):
        acc[...] += lax.dot_general(lanes[p], onehot[p], NT, preferred_element_type=f32)

    per = 4 * ENT // KC

    def near_chunk(h, carry):
        fetch(2 * h, 0, near)
        spread(1)
        fetch(2 * h + 1, 1, near)
        spread(0)
        return carry

    def far_chunk(h, carry):
        fetch(2 * h, 0, far)
        spread(1)
        fetch(2 * h + 1, 1, far)
        spread(0)
        return carry

    lanes[1] = jnp.zeros((256, KC), bf16)
    onehot[1] = jnp.zeros((1024, KC), bf16)
    lax.fori_loop(0, per // 2, near_chunk, 0)
    lax.fori_loop(per // 2, per, far_chunk, 0)
    spread(1)

    for a in range(8):
        at = slice(a * 128, a * 128 + 128)
        tiles[at, :] = (acc[0:128, at] + acc[128:256, at]).T
    for t in range(128):
        i, c = t // 8, t % 8
        melt[i // 8, (i % 8) * 8 : (i % 8) * 8 + 8, c * 128 : c * 128 + 128] = tiles[t * 8 : t * 8 + 8, :]
    mine[...] = melt[core]
    other[...] = melt[1 - core]


def couple(where, packets, thick):
    half = jax.ShapeDtypeStruct((HALF, COLS), f32)
    entry = jax.ShapeDtypeStruct((4, 1, ENT), f32)
    return pl.pallas_call(
        couple_kernel,
        out_shape=(half, half, entry, entry),
        in_specs=[SMEM, VMEM, VMEM],
        out_specs=(VMEM,) * 4,
        scratch_shapes=[
            pltpu.VMEM((1024, 128), f32),
            pltpu.VMEM((256, 1024), bf16),
            pltpu.VMEM((2, 1024, KC), bf16),
            pltpu.VMEM((2, 256, KC), bf16),
            pltpu.VMEM((256, 1024), f32),
            pltpu.VMEM((2, HALF, COLS), f32),
        ],
        cost_estimate=cost(24),
        name="couple",
    )(where, packets, thick)


def ocean_kernel(
    where, temp, uvel, vvel, row_a, row_b, col_a, col_b, col, cav, packet, d0, d1, d2, d3, out
):
    shape = (CX, CY)
    row, lane = sub_iota(shape), lane_iota(shape)
    heat = jnp.zeros((CX, 384), f32)
    for j in range(ENT // KC):
        at = slice(j * KC, (j + 1) * KC)
        draft = d0[0, :, at] + d1[0, :, at] + d2[0, :, at] + d3[0, :, at]
        c = col[0, :, at]
        melt = cav[0, :, at].astype(f32) * melt_rate * (packet[1:2, at] + 0.5 + 0.5 * draft)
        rows = jnp.where(sub_iota((CX, KC)) == (c >> 7), 1.0, 0.0).astype(bf16)
        mask = sub_iota((CY, KC)) == (c & 127)
        parts = [
            jnp.where(mask, part.astype(f32), 0.0).astype(bf16) for part in split3(melt)
        ]
        weights = jnp.concatenate(parts, axis=0)
        heat += lax.dot_general(rows, weights, NT, preferred_element_type=f32)
    column_melt = heat[:, 0:128] + heat[:, 128:256] + heat[:, 256:384]
    even_row, even_col = where[1] == 0, where[3] == 0
    above = jnp.where(even_row, row_a[...], row_b[...])
    below = jnp.where(even_row, row_b[...], row_a[...])
    first_t, second_t = col_a[...].T, col_b[...].T
    east_t = jnp.where(even_col, first_t, second_t)
    west_t = jnp.where(even_col, second_t, first_t)

    def nearby(field, k, side):
        x = field[k]
        e = jnp.where(row == CX - 1, above[side + k : side + k + 1, :], pltpu.roll(x, CX - 1, 0))
        w = jnp.where(row == 0, below[side + k : side + k + 1, :], pltpu.roll(x, 1, 0))
        return x, e, w

    def beside(field, k, side):
        x = field[k]
        n = jnp.where(lane == CY - 1, east_t[:, side + k : side + k + 1], pltpu.roll(x, CY - 1, 1))
        s = jnp.where(lane == 0, west_t[:, side + k : side + k + 1], pltpu.roll(x, 1, 1))
        return x, n, s

    for k in range(LEV):
        t, te, tw = nearby(temp, k, 0)
        _, tn, ts = beside(temp, k, 0)
        u, ue, uw = nearby(uvel, k, 8)
        v, vn, vs = beside(vvel, k, 8)
        speed = 0.5 * (u + ue)
        flux_east = jnp.maximum(speed, 0.0) * t + jnp.minimum(speed, 0.0) * te
        speed = 0.5 * (u + uw)
        flux_west = jnp.maximum(speed, 0.0) * tw + jnp.minimum(speed, 0.0) * t
        speed = 0.5 * (v + vn)
        flux_north = jnp.maximum(speed, 0.0) * t + jnp.minimum(speed, 0.0) * tn
        speed = 0.5 * (v + vs)
        flux_south = jnp.maximum(speed, 0.0) * ts + jnp.minimum(speed, 0.0) * t
        laplace = te + tw + tn + ts - 4.0 * t
        lower = temp[k + 1] - t if k + 1 < LEV else 0.0
        upper = t - temp[k - 1] if k else 0.0
        new = t + flux_west - flux_east + flux_south - flux_north
        new = new + kappa * laplace + vertical_mix * (lower - upper)
        out[k] = new - melt_rate * column_melt if k == 0 else new


def ocean(*arrays):
    return pl.pallas_call(
        ocean_kernel,
        out_shape=jax.ShapeDtypeStruct((LEV, CX, CY), f32),
        in_specs=[SMEM] + [VMEM] * (len(arrays) - 1),
        out_specs=VMEM,
        cost_estimate=cost(3),
        name="ocean",
    )(*arrays)


UP, DOWN, LEFT, RIGHT, INV, SCALE, G = range(7)


def solve_kernel(where, own, partner, near, visc, fric, drive, edge, out, *scratch):
    (vx, fx, sx, k0, k1, k2, v0, v1, v2, f1, f2, g2, res0, res1) = scratch
    core, base = where[1], where[2]
    zero8 = jnp.zeros((8, COLS), f32)

    def put(ref, rows, value):
        if len(ref.shape) == 2:
            ref[rows, :] = value
        else:
            for c in range(8):
                ref[c, rows, :] = value[:, c * 128 : c * 128 + 128]

    def take(ref, rows):
        if len(ref.shape) == 2:
            return ref[rows, :]
        return jnp.concatenate([ref[c, rows, :] for c in range(8)], axis=1)

    for ref in (vx, fx, sx):
        put(ref, slice(0, 8), zero8)
        put(ref, slice(EXT + 8, EXT + 16), zero8)

    for n, (block, full) in enumerate(((visc, vx), (fric, fx), (drive, sx))):

        @pl.when(core == 0)
        def _(n=n, block=block, full=full):
            put(full, slice(8, 72), edge[n])
            put(full, slice(72, 200), block[...])

        @pl.when(core == 1)
        def _(n=n, block=block, full=full):
            put(full, slice(8, 136), block[...])
            put(full, slice(136, 200), edge[n])

    sx[72:136, :] += own[...]

    @pl.when(core == 0)
    def _():
        sx[8:72, :] += near[...]
        sx[136:200, :] += partner[...]

    @pl.when(core == 1)
    def _():
        sx[8:72, :] += partner[...]
        sx[136:200, :] += near[...]

    lane = lane_iota((8, COLS))
    rowi = sub_iota((8, COLS))
    tiles = [EXT // 8 >> level for level in range(LEVELS)]
    ks = (k0, k1, k2)
    vs = (v0, v1, v2)

    def tile(i, d=1):
        if isinstance(i, int):
            return slice(8 * i + 8 * d, 8 * i + 8 * d + 8)
        return pl.ds(pl.multiple_of(8 * i + 8 * d, 8), 8)

    def shifted(ref, i):
        x = take(ref, tile(i))
        above = jnp.where(rowi == 7, take(ref, tile(i, 0)), x)
        below = jnp.where(rowi == 0, take(ref, tile(i, 2)), x)
        return pltpu.roll(above, 1, 0), pltpu.roll(below, 7, 0)

    def loop(lo, hi, body):
        for i in range(lo, hi):
            body(i)

    def left_of(x, s):
        return pltpu.roll(x, s, 1)

    def right_of(x, s):
        return pltpu.roll(x, COLS - s, 1)

    def halved(ref, i, s):
        def at(d):
            return take(ref, pl.ds(16 * i + 8 + d, 8, stride=2))

        pair = at(0) + at(1)
        beside = jnp.where((lane & s) == 0, right_of(pair, s), left_of(pair, s))
        return 0.25 * (pair + beside)

    viscs, frics = (vx, f1, f2), (fx, res1, g2)
    for level in range(LEVELS):
        s = 1 << level
        n = tiles[level]
        kr, vr, fr = ks[level], viscs[level], frics[level]
        if level:

            def coarsen(i, level=level, vr=vr, fr=fr, s=s):
                put(vr, tile(i), halved(viscs[level - 1], i, s // 2))
                put(fr, tile(i), halved(frics[level - 1], i, s // 2))

            put(vr, slice(0, 8), zero8)
            put(vr, slice(n * 8 + 8, n * 8 + 16), zero8)
            for i in range(n):
                coarsen(i)
        scale = 0.5 * 0.25**level
        start = base >> level

        def coefficients(i, level=level, kr=kr, vr=vr, fr=fr, s=s, scale=scale, start=start):
            x = take(vr, tile(i))
            above, below = shifted(vr, i)
            cu = scale * (x + above)
            cd = scale * (x + below)
            cl = scale * (x + jnp.where(lane < s, 0.0, left_of(x, s)))
            cr = scale * (x + jnp.where(lane >= COLS - s, 0.0, right_of(x, s)))
            diag = cu + cd + cl + cr + take(fr, tile(i))
            row = start + 8 * i + rowi
            inside = (row >= 0) & (row < (COLS >> level))
            inv = jnp.where(inside, omega / diag, 0.0)
            kr[UP, tile(i), :] = inv * cu
            kr[DOWN, tile(i), :] = inv * cd
            kr[LEFT, tile(i), :] = jnp.where(lane < s, 0.0, inv * cl)
            kr[RIGHT, tile(i), :] = jnp.where(lane >= COLS - s, 0.0, inv * cr)
            kr[SCALE, tile(i), :] = jnp.where(inside, diag * (1.0 / omega), 0.0)
            kr[INV, tile(i), :] = inv
            if level == 0:
                kr[G, tile(i), :] = inv * sx[tile(i), :]

        loop(0, n, coefficients)

    def step_of(level, src, i):
        kr, s = ks[level], 1 << level
        v = src[tile(i), :]
        above, below = shifted(src, i)
        total = kr[G, tile(i), :] + kr[UP, tile(i), :] * above + kr[DOWN, tile(i), :] * below
        total = total + kr[LEFT, tile(i), :] * left_of(v, s)
        total = total + kr[RIGHT, tile(i), :] * right_of(v, s)
        return v, total - omega * v

    def core_tiles(level, h):
        n = tiles[level]
        return max(n // 3 - h, 0), min(2 * n // 3 + h, n)

    def sweep(level, a, b, h):
        src, dst = vs[level].at[a], vs[level].at[b]

        def body(i):
            v, t = step_of(level, src, i)
            dst[tile(i), :] = v + t

        loop(*core_tiles(level, h), body)

    def residual(level, a, h, res):
        src = vs[level].at[a]

        def body(i):
            _, t = step_of(level, src, i)
            put(res, tile(i), t * ks[level][SCALE, tile(i), :])

        loop(*core_tiles(level, h), body)

    def free_sweep(level, a, h, source, s):
        kr, dst = ks[level], vs[level].at[a]

        def body(i):
            if source is not None:
                kr[G, tile(i), :] = kr[INV, tile(i), :] * halved(source, i, s)
            dst[tile(i), :] = kr[G, tile(i), :]

        if source is None:
            loop(*core_tiles(level, h), body)
            return
        for i in range(*core_tiles(level, h)):
            body(i)

    def correct(level, a, b, h, spread):
        fine, coarse = vs[level].at[a], vs[level + 1].at[b]
        lo, hi = core_tiles(level, h)

        def widen(i):
            e = coarse[tile(i), :]
            put(spread, pl.ds(16 * i + 8, 8, stride=2), e)
            put(spread, pl.ds(16 * i + 9, 8, stride=2), e)

        for i in range(lo // 2, (hi + 1) // 2):
            widen(i)

        def add(i):
            fine[tile(i), :] += take(spread, tile(i))

        loop(lo, hi, add)

    def clear(ref, i):
        put(ref, tile(i, 0), zero8)

    for level in range(LEVELS):
        for a in range(2):
            loop(0, tiles[level] + 2, functools.partial(clear, vs[level].at[a]))
    loop(0, tiles[0] + 2, functools.partial(clear, res0))
    loop(0, tiles[1] + 2, functools.partial(clear, res1))

    for cycle in range(CYCLES):
        first = cycle == 0
        now = 1
        if first:
            free_sweep(0, 0, 8, None, 1)
        else:
            sweep(0, 1, 0, 4)
        sweep(0, 0, 1, 8 if first else 4)
        residual(0, now, 7 if first else 4, res0)
        free_sweep(1, 0, 4 if first else 2, res0, 1)
        sweep(1, 0, 1, 4 if first else 2)
        residual(1, 1, 3 if first else 2, res1)
        h2 = 2 if first else 1
        free_sweep(2, 0, h2, res1, 2)
        sweep(2, 0, 1, h2)
        sweep(2, 1, 0, h2)
        sweep(2, 0, 1, h2)
        correct(1, 1, 1, 3 if first else 1, f1)
        sweep(1, 1, 0, 3 if first else 1)
        sweep(1, 0, 1, 3 if first else 1)
        correct(0, now, 1, 4 if first else 1, vx)
        sweep(0, now, 1 - now, 4 if first else 1)
        sweep(0, 1 - now, now, 4 if first else 0)
    out[...] = v0[1, 72:136, :]


def solve(where, own, partner, near, visc, fric, drive, edge):
    def rows(level, *lead):
        return pltpu.VMEM((*lead, (EXT >> level) + 16, COLS), f32)

    def blocks(level):
        return pltpu.VMEM((8, (EXT >> level) + 16, 128), f32)

    return pl.pallas_call(
        solve_kernel,
        out_shape=jax.ShapeDtypeStruct((HALF, COLS), f32),
        in_specs=[SMEM] + [VMEM] * 7,
        out_specs=VMEM,
        scratch_shapes=[
            blocks(0),
            blocks(0),
            rows(0),
            rows(0, 7),
            rows(1, 7),
            rows(2, 7),
            rows(0, 2),
            rows(1, 2),
            rows(2, 2),
            blocks(1),
            rows(2),
            rows(2),
            blocks(0),
            blocks(1),
        ],
        cost_estimate=cost(10),
        name="solve",
    )(where, own, partner, near, visc, fric, drive, edge)


def flip(n, k):
    return [(i, i ^ k) for i in range(n)]


def pairs(n, turn):
    later = [(i, i + 1) for i in range(turn, n - 1, 2)]
    return later + [(b, a) for a, b in later]


def step(temp, uvel, vvel, col, cell, cav, thick, visc, fric, drive):
    core = lax.axis_index("co").astype(i32)
    y = lax.axis_index("y").astype(i32)
    blk = lax.axis_index("xh").astype(i32) * 4 + y
    where = jnp.stack([blk * CELLS, core, blk * ROWS + core * HALF - 64, y & 1])

    packet, row_a, row_b, col_a, col_b = pack(where, temp, uvel, vvel, col, cell, cav)
    got = [packet] + [lax.ppermute(packet, "y", flip(4, k)) for k in range(1, 4)]
    got = jnp.stack(got)
    packets = jnp.concatenate([got, lax.ppermute(got, "xh", flip(2, 1))], axis=0)

    ring = ("co", "xh", "y")
    outer = [(b, 8 + b - 1) for b in range(1, 8)] + [(8 + b, b + 1) for b in range(7)]
    ice = jnp.stack([visc, fric, drive])
    ice_edge = lax.dynamic_slice_in_dim(ice, core * HALF, HALF, axis=1)
    edge = lax.ppermute(ice_edge, ring, outer)
    row_a = lax.ppermute(row_a, "co", flip(2, 1))
    row_b = lax.ppermute(row_b, GRP, pairs(16, 1))
    col_a = lax.ppermute(col_a, "y", flip(4, 1))
    col_b = lax.ppermute(col_b, BLK, pairs(8, 1))

    mine, other, close, far = couple(where, packets, thick)
    mine = mine + lax.ppermute(other, "co", flip(2, 1))
    far = lax.ppermute(far, "xh", flip(2, 1))
    parts = lax.all_to_all(mine.reshape(8, 8, COLS), ZX, 0, 0, tiled=True)
    total = parts.sum(axis=0)
    own = lax.all_to_all(jnp.broadcast_to(total[None], (8, 8, COLS)), ZX, 0, 0, tiled=True)
    own = own.reshape(HALF, COLS)
    partner = lax.ppermute(own, "co", flip(2, 1))
    near = lax.ppermute(own, ring, outer)
    close = close + far
    back = [lax.ppermute(close[k], "y", flip(4, k))[None] for k in range(1, 4)]
    half = solve(where, own, partner, near, visc, fric, drive, edge)
    rest = lax.ppermute(half, "co", flip(2, 1))
    temp_new = ocean(
        where, temp, uvel, vvel, row_a, row_b, col_a, col_b, col, cav, packet,
        close[0:1], *back,
    )
    first = core == 0
    ice_velocity = jnp.concatenate(
        [jnp.where(first, half, rest), jnp.where(first, rest, half)], axis=0
    )
    return temp_new, ice_velocity


def solution(mesh):
    finer = Mesh(mesh.devices.reshape(4, 2, 2, 2, 4), ("z", "xl", "co", "xh", "y"))
    field = P(None, GRP, BLK)
    entry = P(GRP, BLK, None)
    rows = P(BLK, None)
    return jax.shard_map(
        step,
        mesh=finer,
        in_specs=(field,) * 3 + (entry,) * 3 + (rows,) * 4,
        out_specs=(field, rows),
        check_vma=False,
    )
```

profile of v0, /device:TPU:6, one launch (start us, length us, event | category | flops | bytes accessed | tf_op | source)
XLA Modules:
  0.0 115.5 jit_solution(7586502009834504764)
XLA Ops:
  1.3 2.4 %pack.1 = (f32[2,2048]{1,0:T(2,128)}, f32[16,128]{1,0:T(8,128)}, f32[16,128]{1,0:T(8,128)}, f32[16,64]{1,0:T(8,128)}, f32[16,64]{1,0:T(8,128)}) custom-call(s32[4]{0:T(128)} %pad_add_fusion.where, f32[8,64,128]{2,1,0:T(8,128)} %temp.3, f32[8,64,128]{2,1,0:T(8,128)} %uvel.3, f32[8,64,128]{2,1,0:T(8,128)} %vvel.3, s32[1,1,2048]{2,1,0:T(1,128)} %col.3, ...), custom_call_target="tpu_custom_call" | custom-call | flops 60000000 | tf_op jit(solution)/shard_map/pack/pallas_call | solution.py:94
  3.7 1.6 %collective-permute-start.4 = (f32[2,2048]{1,0:T(2,128)}, f32[2,2048]{1,0:T(2,128)S(1)}, u32[]{:S(2)}, u32[]{:S(2)}) collective-permute-start(f32[2,2048]{1,0:T(2,128)} %get-tuple-element.15.packet), channel_id=1, source_target_pairs={{0,1},{1,0},{2,3},{3,2},{4,5},{5,4},{6,7},{7,6},{8,9},{9,8},{10,11... | collective-permute-start | bytes 49160 | tf_op jit(solution)/shard_map/ppermute | solution.py:542
  5.3 2.9 %collective-permute-start.5 = (f32[2,2048]{1,0:T(2,128)}, f32[2,2048]{1,0:T(2,128)S(1)}, u32[]{:S(2)}, u32[]{:S(2)}) collective-permute-start(f32[2,2048]{1,0:T(2,128)} %get-tuple-element.15.packet), channel_id=1, source_target_pairs={{0,2},{1,3},{2,0},{3,1},{4,6},{5,7},{6,4},{7,5},{8,10},{9,11},{10,... | collective-permute-start | bytes 49160 | tf_op jit(solution)/shard_map/ppermute | solution.py:542
  8.4 0.8 constant_dynamic-update-slice_fusion.4
  9.1 1.6 %collective-permute-done.5 = f32[2,2048]{1,0:T(2,128)S(1)} collective-permute-done((f32[2,2048]{1,0:T(2,128)}, f32[2,2048]{1,0:T(2,128)S(1)}, u32[]{:S(2)}, u32[]{:S(2)}) %collective-permute-start.5) | collective-permute-done | bytes 16416 | tf_op jit(solution)/shard_map/ppermute | solution.py:542
  10.7 2.6 %collective-permute-done.6 = f32[2,2048]{1,0:T(2,128)S(1)} collective-permute-done((f32[2,2048]{1,0:T(2,128)}, f32[2,2048]{1,0:T(2,128)S(1)}, u32[]{:S(2)}, u32[]{:S(2)}) %collective-permute-start.6) | collective-permute-done | bytes 16416 | tf_op jit(solution)/shard_map/ppermute | solution.py:542
  13.3 0.7 pad_maximum_fusion.1
  14.1 1.5 %collective-permute-start.7 = (f32[4,2,2048]{2,1,0:T(2,128)S(1)}, f32[4,2,2048]{2,1,0:T(2,128)S(1)}, u32[]{:S(2)}, u32[]{:S(2)}) collective-permute-start(f32[4,2,2048]{2,1,0:T(2,128)S(1)} %pad_maximum_fusion.1), channel_id=1, source_target_pairs={{0,4},{4,0},{1,5},{5,1},{2,6},{6,2},{3,7},{7,3},{8,12},{12,8},{9,1... | collective-permute-start | bytes 196616 | tf_op jit(solution)/shard_map/ppermute | solution.py:544
  15.6 4.3 %collective-permute-done.7 = f32[4,2,2048]{2,1,0:T(2,128)S(1)} collective-permute-done((f32[4,2,2048]{2,1,0:T(2,128)S(1)}, f32[4,2,2048]{2,1,0:T(2,128)S(1)}, u32[]{:S(2)}, u32[]{:S(2)}) %collective-permute-start.7) | collective-permute-done | bytes 65568 | tf_op jit(solution)/shard_map/ppermute | solution.py:544
  20.6 24.2 %couple.1 = (f32[64,1024]{1,0:T(8,128)}, f32[64,1024]{1,0:T(8,128)}, f32[4,1,2048]{2,1,0:T(1,128)}, f32[4,1,2048]{2,1,0:T(1,128)}) custom-call(s32[4]{0:T(128)} %pad_add_fusion.where, f32[8,2,2048]{2,1,0:T(2,128)} %copy-done.17, f32[128,1024]{1,0:T(8,128)} %thick.1), custom_call_target="tpu_custom_call" | custom-call | flops 480000000 | tf_op jit(solution)/shard_map/couple/pallas_call | solution.py:185
  45.0 3.1 %collective-permute-start.15 = (f32[3,64,1024]{2,1,0:T(8,128)S(1)}, f32[3,64,1024]{2,1,0:T(8,128)S(1)}, u32[]{:S(2)}, u32[]{:S(2)}) collective-permute-start(f32[3,64,1024]{2,1,0:T(8,128)S(1)} %fusion.1), channel_id=1, source_target_pairs={{1,8},{2,9},{3,10},{4,11},{5,12},{6,13},{7,14},{8,1},{9,2},{10,3},... | collective-permute-start | bytes 2359304 | tf_op jit(solution)/shard_map/ppermute | solution.py:550
  48.2 15.7 %all_to_all.10 = f32[8,8,1024]{2,1,0:T(8,128)S(1)} all-to-all(f32[8,8,1024]{2,1,0:T(8,128)S(1)} %add_bitcast_fusion), channel_id=1, replica_groups=mesh['z'=4,'xl'=2,'co'=2,'xh'=2,'y'=4] {'z','xl'}, dimensions={0} | all-to-all | bytes 524288 | tf_op jit(solution)/shard_map/all_to_all | solution.py:559
  63.9 11.0 %all_to_all.11 = f32[8,8,1024]{2,1,0:T(8,128)S(1)} all-to-all(f32[8,8,1024]{2,1,0:T(8,128)S(1)} %broadcast_in_dim.18), channel_id=1, replica_groups=mesh['z'=4,'xl'=2,'co'=2,'xh'=2,'y'=4] {'z','xl'}, dimensions={0} | all-to-all | bytes 524288 | tf_op jit(solution)/shard_map/all_to_all | solution.py:561
  74.9 4.1 %collective-permute-start.14 = (f32[64,1024]{1,0:T(8,128)S(1)}, f32[64,1024]{1,0:T(8,128)S(1)}, u32[]{:S(2)}, u32[]{:S(2)}) collective-permute-start(f32[64,1024]{1,0:T(8,128)S(1)} %bitcast.31), channel_id=1, source_target_pairs={{1,8},{2,9},{3,10},{4,11},{5,12},{6,13},{7,14},{8,1},{9,2},{10,3},... | collective-permute-start | bytes 786440 | tf_op jit(solution)/shard_map/ppermute | solution.py:564
  79.2 5.3 %collective-permute-done.8 = f32[4,1,2048]{2,1,0:T(1,128)S(1)} collective-permute-done((f32[4,1,2048]{2,1,0:T(1,128)S(1)}, f32[4,1,2048]{2,1,0:T(1,128)S(1)}, u32[]{:S(2)}, u32[]{:S(2)}) %collective-permute-start.8) | collective-permute-done | bytes 32800 | tf_op jit(solution)/shard_map/ppermute | solution.py:558
  84.5 1.9 %collective-permute-start.1 = (f32[16,128]{1,0:T(8,128)S(1)}, f32[16,128]{1,0:T(8,128)S(1)}, u32[]{:S(2)}, u32[]{:S(2)}) collective-permute-start(f32[16,128]{1,0:T(8,128)S(1)} %copy-done.19), channel_id=1, source_target_pairs={{8,16},{24,32},{40,48},{56,64},{72,80},{88,96},{104,112},{16,8},{3... | collective-permute-start | bytes 24584 | tf_op jit(solution)/shard_map/ppermute | solution.py:552
  86.6 5.7 %collective-permute-start.3 = (f32[16,64]{1,0:T(8,128)S(1)}, f32[16,64]{1,0:T(8,128)S(1)}, u32[]{:S(2)}, u32[]{:S(2)}) collective-permute-start(f32[16,64]{1,0:T(8,128)S(1)} %copy-done.21), channel_id=1, source_target_pairs={{1,2},{3,4},{5,6},{2,1},{4,3},{6,5},{9,10},{11,12},{13,14},{10,9},... | collective-permute-start | bytes 12296 | tf_op jit(solution)/shard_map/ppermute | solution.py:554
  93.0 10.3 %solve.1 = f32[64,1024]{1,0:T(8,128)} custom-call(s32[4]{0:T(128)} %pad_add_fusion.where, f32[64,1024]{1,0:T(8,128)} %bitcast.32, f32[64,1024]{1,0:T(8,128)} %copy-done.6, f32[64,1024]{1,0:T(8,128)} %copy-done.7, f32[128,1024]{1,0:T(8,128)} %visc.1, f32[128,1024]{1,0:T(8,128)} %fric.1, f32[128,1024]{1,0:T(8,128)} %drive.1, f32[3,64,1024]{2,1,0:T(8,128)} %copy-done.5), custom_call_target="tpu_custom_call" | custom-call | flops 200000000 | tf_op jit(solution)/shard_map/solve/pallas_call | solution.py:500
  104.0 0.8 collective-permute-start.10
  104.8 2.6 %collective-permute-start.11 = (f32[1,2048]{1,0:T(1,128)S(1)}, f32[1,2048]{1,0:T(1,128)S(1)}, u32[]{:S(2)}, u32[]{:S(2)}) collective-permute-start(f32[1,2048]{1,0:T(1,128)S(1)} %get-tuple-element.22), channel_id=1, source_target_pairs={{0,3},{1,2},{2,1},{3,0},{4,7},{5,6},{6,5},{7,4},{8,11},{9,10},{10,... | collective-permute-start | bytes 24584 | tf_op jit(solution)/shard_map/ppermute | solution.py:566
  107.5 1.6 %collective-permute-done.10 = f32[1,2048]{1,0:T(1,128)S(1)} collective-permute-done((f32[1,2048]{1,0:T(1,128)S(1)}, f32[1,2048]{1,0:T(1,128)S(1)}, u32[]{:S(2)}, u32[]{:S(2)}) %collective-permute-start.10) | collective-permute-done | bytes 8224 | tf_op jit(solution)/shard_map/ppermute | solution.py:566
  109.7 1.4 %collective-permute-done.9 = f32[1,2048]{1,0:T(1,128)S(1)} collective-permute-done((f32[1,2048]{1,0:T(1,128)S(1)}, f32[1,2048]{1,0:T(1,128)S(1)}, u32[]{:S(2)}, u32[]{:S(2)}) %collective-permute-start.9) | collective-permute-done | bytes 8224 | tf_op jit(solution)/shard_map/ppermute | solution.py:566
  111.7 2.8 %ocean.1 = f32[8,64,128]{2,1,0:T(8,128)} custom-call(s32[4]{0:T(128)} %pad_add_fusion.where, f32[8,64,128]{2,1,0:T(8,128)} %temp.3, f32[8,64,128]{2,1,0:T(8,128)} %uvel.3, f32[8,64,128]{2,1,0:T(8,128)} %vvel.3, f32[16,128]{1,0:T(8,128)} %copy-done.10, f32[16,128]{1,0:T(8,128)} %copy-done.11, f32[16,64]{1,0:T(8,128)} %copy-done.12, f32[16,64]{1,0:T(8,128)} %copy-done.13, ...), custom_call_target="tpu_custom_call" | custom-call | flops 60000000 | tf_op jit(solution)/shard_map/ocean/pallas_call | solution.py:263
  114.6 0.8 pad_maximum_fusion
  (77 shorter events, 4.6 us)
Async XLA Ops:
  3.7 5.5 %collective-permute-start.4 = (f32[2,2048]{1,0:T(2,128)}, f32[2,2048]{1,0:T(2,128)S(1)}, u32[]{:S(2)}, u32[]{:S(2)}) collective-permute-start(f32[2,2048]{1,0:T(2,128)} %get-tuple-element.15.packet), channel_id=1, source_target_pairs={{0,1},{1,0},{2,3},{3,2},{4,5},{5,4},{6,7},{7,6},{8,9},{9,8},{10,11... | collective-permute-start | bytes 49160 | tf_op jit(solution)/shard_map/ppermute | solution.py:542
  5.3 5.5 %collective-permute-start.5 = (f32[2,2048]{1,0:T(2,128)}, f32[2,2048]{1,0:T(2,128)S(1)}, u32[]{:S(2)}, u32[]{:S(2)}) collective-permute-start(f32[2,2048]{1,0:T(2,128)} %get-tuple-element.15.packet), channel_id=1, source_target_pairs={{0,2},{1,3},{2,0},{3,1},{4,6},{5,7},{6,4},{7,5},{8,10},{9,11},{10,... | collective-permute-start | bytes 49160 | tf_op jit(solution)/shard_map/ppermute | solution.py:542
  8.2 5.2 %collective-permute-start.6 = (f32[2,2048]{1,0:T(2,128)}, f32[2,2048]{1,0:T(2,128)S(1)}, u32[]{:S(2)}, u32[]{:S(2)}) collective-permute-start(f32[2,2048]{1,0:T(2,128)} %get-tuple-element.15.packet), channel_id=1, source_target_pairs={{0,3},{1,2},{2,1},{3,0},{4,7},{5,6},{6,5},{7,4},{8,11},{9,10},{10,... | collective-permute-start | bytes 49160 | tf_op jit(solution)/shard_map/ppermute | solution.py:542
  14.1 5.8 %collective-permute-start.7 = (f32[4,2,2048]{2,1,0:T(2,128)S(1)}, f32[4,2,2048]{2,1,0:T(2,128)S(1)}, u32[]{:S(2)}, u32[]{:S(2)}) collective-permute-start(f32[4,2,2048]{2,1,0:T(2,128)S(1)} %pad_maximum_fusion.1), channel_id=1, source_target_pairs={{0,4},{4,0},{1,5},{5,1},{2,6},{6,2},{3,7},{7,3},{8,12},{12,8},{9,1... | collective-permute-start | bytes 196616 | tf_op jit(solution)/shard_map/ppermute | solution.py:544
  20.6 24.3 %copy-start.2 = (f32[128,1024]{1,0:T(8,128)S(1)}, f32[128,1024]{1,0:T(8,128)}, u32[]{:S(2)}) copy-start(f32[128,1024]{1,0:T(8,128)} %drive.1) | copy-start | bytes 1572868
  44.8 3.2 %collective-permute-start.12 = (f32[64,1024]{1,0:T(8,128)}, f32[64,1024]{1,0:T(8,128)S(1)}, u32[]{:S(2)}, u32[]{:S(2)}) collective-permute-start(f32[64,1024]{1,0:T(8,128)} %get-tuple-element.19), channel_id=1, source_target_pairs={{0,8},{8,0},{1,9},{9,1},{2,10},{10,2},{3,11},{11,3},{4,12},{12,4},... | collective-permute-start | bytes 786440 | tf_op jit(solution)/shard_map/ppermute | solution.py:557
  45.0 41.5 %collective-permute-start.15 = (f32[3,64,1024]{2,1,0:T(8,128)S(1)}, f32[3,64,1024]{2,1,0:T(8,128)S(1)}, u32[]{:S(2)}, u32[]{:S(2)}) collective-permute-start(f32[3,64,1024]{2,1,0:T(8,128)S(1)} %fusion.1), channel_id=1, source_target_pairs={{1,8},{2,9},{3,10},{4,11},{5,12},{6,13},{7,14},{8,1},{9,2},{10,3},... | collective-permute-start | bytes 2359304 | tf_op jit(solution)/shard_map/ppermute | solution.py:550
  48.1 30.9 %copy-start.18 = (f32[4,1,2048]{2,1,0:T(1,128)S(1)}, f32[4,1,2048]{2,1,0:T(1,128)}, u32[]{:S(2)}) copy-start(f32[4,1,2048]{2,1,0:T(1,128)} %get-tuple-element.17) | copy-start | bytes 98308
  48.1 30.9 %copy-start.20 = (f32[16,128]{1,0:T(8,128)S(1)}, f32[16,128]{1,0:T(8,128)}, u32[]{:S(2)}) copy-start(f32[16,128]{1,0:T(8,128)} %get-tuple-element.11) | copy-start | bytes 24580
  48.1 36.3 %copy-start.19 = (f32[16,128]{1,0:T(8,128)S(1)}, f32[16,128]{1,0:T(8,128)}, u32[]{:S(2)}) copy-start(f32[16,128]{1,0:T(8,128)} %get-tuple-element.12) | copy-start | bytes 24580
  48.1 38.3 %copy-start.9 = (f32[4,1,2048]{2,1,0:T(1,128)S(1)}, f32[4,1,2048]{2,1,0:T(1,128)}, u32[]{:S(2)}) copy-start(f32[4,1,2048]{2,1,0:T(1,128)} %get-tuple-element.16) | copy-start | bytes 98308
  48.1 38.3 %copy-start.22 = (f32[16,64]{1,0:T(8,128)S(1)}, f32[16,64]{1,0:T(8,128)}, u32[]{:S(2)}) copy-start(f32[16,64]{1,0:T(8,128)} %get-tuple-element.13) | copy-start | bytes 12292
  48.2 38.4 %copy-start.21 = (f32[16,64]{1,0:T(8,128)S(1)}, f32[16,64]{1,0:T(8,128)}, u32[]{:S(2)}) copy-start(f32[16,64]{1,0:T(8,128)} %get-tuple-element.14) | copy-start | bytes 12292
  74.9 11.7 %collective-permute-start.13 = (f32[64,1024]{1,0:T(8,128)S(1)}, f32[64,1024]{1,0:T(8,128)S(1)}, u32[]{:S(2)}, u32[]{:S(2)}) collective-permute-start(f32[64,1024]{1,0:T(8,128)S(1)} %bitcast.30), channel_id=1, source_target_pairs={{0,8},{8,0},{1,9},{9,1},{2,10},{10,2},{3,11},{11,3},{4,12},{12,4},... | collective-permute-start | bytes 786440 | tf_op jit(solution)/shard_map/ppermute | solution.py:563
  74.9 17.4 %collective-permute-start.14 = (f32[64,1024]{1,0:T(8,128)S(1)}, f32[64,1024]{1,0:T(8,128)S(1)}, u32[]{:S(2)}, u32[]{:S(2)}) collective-permute-start(f32[64,1024]{1,0:T(8,128)S(1)} %bitcast.31), channel_id=1, source_target_pairs={{1,8},{2,9},{3,10},{4,11},{5,12},{6,13},{7,14},{8,1},{9,2},{10,3},... | collective-permute-start | bytes 786440 | tf_op jit(solution)/shard_map/ppermute | solution.py:564
  79.0 5.5 %collective-permute-start.8 = (f32[4,1,2048]{2,1,0:T(1,128)S(1)}, f32[4,1,2048]{2,1,0:T(1,128)S(1)}, u32[]{:S(2)}, u32[]{:S(2)}) collective-permute-start(f32[4,1,2048]{2,1,0:T(1,128)S(1)} %copy-done.18), channel_id=1, source_target_pairs={{0,4},{4,0},{1,5},{5,1},{2,6},{6,2},{3,7},{7,3},{8,12},{12,8},{9,1... | collective-permute-start | bytes 98312 | tf_op jit(solution)/shard_map/ppermute | solution.py:558
  79.1 28.4 %collective-permute-start = (f32[16,128]{1,0:T(8,128)S(1)}, f32[16,128]{1,0:T(8,128)S(1)}, u32[]{:S(2)}, u32[]{:S(2)}) collective-permute-start(f32[16,128]{1,0:T(8,128)S(1)} %copy-done.20), channel_id=1, source_target_pairs={{0,8},{8,0},{1,9},{9,1},{2,10},{10,2},{3,11},{11,3},{4,12},{12,4},... | collective-permute-start | bytes 24584 | tf_op jit(solution)/shard_map/ppermute | solution.py:551
  84.5 23.0 %collective-permute-start.1 = (f32[16,128]{1,0:T(8,128)S(1)}, f32[16,128]{1,0:T(8,128)S(1)}, u32[]{:S(2)}, u32[]{:S(2)}) collective-permute-start(f32[16,128]{1,0:T(8,128)S(1)} %copy-done.19), channel_id=1, source_target_pairs={{8,16},{24,32},{40,48},{56,64},{72,80},{88,96},{104,112},{16,8},{3... | collective-permute-start | bytes 24584 | tf_op jit(solution)/shard_map/ppermute | solution.py:552
  86.5 17.5 %collective-permute-start.2 = (f32[16,64]{1,0:T(8,128)S(1)}, f32[16,64]{1,0:T(8,128)S(1)}, u32[]{:S(2)}, u32[]{:S(2)}) collective-permute-start(f32[16,64]{1,0:T(8,128)S(1)} %copy-done.22), channel_id=1, source_target_pairs={{0,1},{1,0},{2,3},{3,2},{4,5},{5,4},{6,7},{7,6},{8,9},{9,8},{10,11... | collective-permute-start | bytes 12296 | tf_op jit(solution)/shard_map/ppermute | solution.py:553
  86.6 18.2 %collective-permute-start.3 = (f32[16,64]{1,0:T(8,128)S(1)}, f32[16,64]{1,0:T(8,128)S(1)}, u32[]{:S(2)}, u32[]{:S(2)}) collective-permute-start(f32[16,64]{1,0:T(8,128)S(1)} %copy-done.21), channel_id=1, source_target_pairs={{1,2},{3,4},{5,6},{2,1},{4,3},{6,5},{9,10},{11,12},{13,14},{10,9},... | collective-permute-start | bytes 12296 | tf_op jit(solution)/shard_map/ppermute | solution.py:554
  103.4 11.2 %collective-permute-start.16 = (f32[64,1024]{1,0:T(8,128)}, f32[64,1024]{1,0:T(8,128)S(1)}, u32[]{:S(2)}, u32[]{:S(2)}) collective-permute-start(f32[64,1024]{1,0:T(8,128)} %solve.1), channel_id=1, source_target_pairs={{0,8},{8,0},{1,9},{9,1},{2,10},{10,2},{3,11},{11,3},{4,12},{12,4},... | collective-permute-start | bytes 786440 | tf_op jit(solution)/shard_map/ppermute | solution.py:568
  104.0 5.2 %collective-permute-start.10 = (f32[1,2048]{1,0:T(1,128)S(1)}, f32[1,2048]{1,0:T(1,128)S(1)}, u32[]{:S(2)}, u32[]{:S(2)}) collective-permute-start(f32[1,2048]{1,0:T(1,128)S(1)} %get-tuple-element.23), channel_id=1, source_target_pairs={{0,2},{1,3},{2,0},{3,1},{4,6},{5,7},{6,4},{7,5},{8,10},{9,11},{10,... | collective-permute-start | bytes 24584 | tf_op jit(solution)/shard_map/ppermute | solution.py:566
  104.8 4.9 %collective-permute-start.11 = (f32[1,2048]{1,0:T(1,128)S(1)}, f32[1,2048]{1,0:T(1,128)S(1)}, u32[]{:S(2)}, u32[]{:S(2)}) collective-permute-start(f32[1,2048]{1,0:T(1,128)S(1)} %get-tuple-element.22), channel_id=1, source_target_pairs={{0,3},{1,2},{2,1},{3,0},{4,7},{5,6},{6,5},{7,4},{8,11},{9,10},{10,... | collective-permute-start | bytes 24584 | tf_op jit(solution)/shard_map/ppermute | solution.py:566
  107.4 3.7 %collective-permute-start.9 = (f32[1,2048]{1,0:T(1,128)S(1)}, f32[1,2048]{1,0:T(1,128)S(1)}, u32[]{:S(2)}, u32[]{:S(2)}) collective-permute-start(f32[1,2048]{1,0:T(1,128)S(1)} %get-tuple-element.24), channel_id=1, source_target_pairs={{0,1},{1,0},{2,3},{3,2},{4,5},{5,4},{6,7},{7,6},{8,9},{9,8},{10,11... | collective-permute-start | bytes 24584 | tf_op jit(solution)/shard_map/ppermute | solution.py:566
  (16 other events, 118.1 us)
where the time goes:
time: 116 us; the launch traced here: 115 us
  Pallas kernels  39.8 us (34%)
  blocking collectives  26.6 us (23%)
  starting transfers between devices  24.7 us (21%)
  waiting for transfers between devices  17.5 us (15%)
  local copies, waits for them, and re-layouts  3.37 us (3%)
  other arithmetic  2.46 us (2%)
    pallas_call x1, Pallas kernels, couple(): pl.pallas_call(couple_kernel, out_shape=(half, half, entry, entry), in_sp...  24.2 us
    all_to_all x1, blocking collectives, step(): parts = lax.all_to_all(mine.reshape(8, 8, COLS), ZX, 0, 0, tiled=True)  15.7 us
    all_to_all x1, blocking collectives, step(): lax.all_to_all(jnp.broadcast_to(total[None], (8, 8, COLS)), ZX, 0, 0, til...  11 us
    pallas_call x1, Pallas kernels, solve(): pl.pallas_call(solve_kernel, out_shape=jax.ShapeDtypeStruct((HALF, COLS),...  10.3 us
    ppermute x1, starting transfers between devices, step(): col_b = lax.ppermute(col_b, BLK, pairs(8, 1))  5.7 us
    ppermute x1, waiting for transfers between devices, step(): far = lax.ppermute(far, 'xh', flip(2, 1))  5.3 us
    ppermute x3, starting transfers between devices, step(): lax.ppermute(packet, 'y', flip(4, k))  4.7 us
    ppermute x1, waiting for transfers between devices, step(): lax.ppermute(got, 'xh', flip(2, 1))  4.34 us
  transfers between devices with their start and end apart: 17, of which 7 were waited for; matrix products, arithmetic and copies ran while one was open for 1% of the time, Pallas kernels for 11%

commit v1 on v0

--- a/solution.py
+++ b/solution.py
@@ -11,7 +11,6 @@
 LEVELS = 3
 CYCLES = 2
 GRP = ("z", "xl", "co")
-ZX = ("z", "xl")
 BLK = ("xh", "y")
 omega = 0.8
 kappa = 0.1
@@ -554,16 +553,23 @@
     col_b = lax.ppermute(col_b, BLK, pairs(8, 1))
 
     mine, other, close, far = couple(where, packets, thick)
-    mine = mine + lax.ppermute(other, "co", flip(2, 1))
+    theirs = lax.ppermute(other, "co", flip(2, 1))
     far = lax.ppermute(far, "xh", flip(2, 1))
-    parts = lax.all_to_all(mine.reshape(8, 8, COLS), ZX, 0, 0, tiled=True)
-    total = parts.sum(axis=0)
-    own = lax.all_to_all(jnp.broadcast_to(total[None], (8, 8, COLS)), ZX, 0, 0, tiled=True)
-    own = own.reshape(HALF, COLS)
+    part_a = mine[:32] + theirs[:32]
+    part_b = mine[32:] + theirs[32:]
+    ways = {"xl": flip(2, 1), "z": flip(4, 1)}
+    around = [(i, 3 - i) for i in range(4)]
+    part_a = part_a + lax.ppermute(part_a, "xl", ways["xl"])
+    part_b = part_b + lax.ppermute(part_b, "z", ways["z"])
+    part_a = part_a + lax.ppermute(part_a, "z", ways["z"])
+    part_b = part_b + lax.ppermute(part_b, "z", around)
+    close = close + far
+    back = [lax.ppermute(close[k], "y", flip(4, k))[None] for k in range(1, 4)]
+    part_a = part_a + lax.ppermute(part_a, "z", around)
+    part_b = part_b + lax.ppermute(part_b, "xl", ways["xl"])
+    own = jnp.concatenate([part_a, part_b], axis=0)
     partner = lax.ppermute(own, "co", flip(2, 1))
     near = lax.ppermute(own, ring, outer)
-    close = close + far
-    back = [lax.ppermute(close[k], "y", flip(4, k))[None] for k in range(1, 4)]
     half = solve(where, own, partner, near, visc, fric, drive, edge)
     rest = lax.ppermute(half, "co", flip(2, 1))
     temp_new = ocean(

time: 116 us -> 117 us (level)
  blocking collectives: 26.6 us -> 0 us
  starting transfers between devices: 24.7 us -> 38.6 us
  waiting for transfers between devices: 17.5 us -> 31.2 us
    all_to_all x2 -> x0, blocking collectives: 26.6 us -> none  [the longest x1 15.7 us: step(): parts = lax.all_to_all(mine.reshape(8, 8, COLS), ZX, 0, 0, tiled=True)]
    ppermute x1 -> x7, waiting for transfers between devices: 0.01 us -> 13.8 us  [the longest x1 10.4 us: step(): part_a = part_a + lax.ppermute(part_a, 'xl', ways['xl'])]
    ppermute x1 -> x7, starting transfers between devices: 0.01 us -> 13 us  [the longest x1 4.21 us: step(): part_a = part_a + lax.ppermute(part_a, 'z', around)]
  transfers between devices with their start and end apart: 17 -> 23, of which waited for: 7 -> 11; matrix products, arithmetic and copies ran while one was open for 1% -> 1% of each run, Pallas kernels for 11% -> 11%
where the time goes in v1:
time: 117 us
  Pallas kernels  39.8 us (34%)
  starting transfers between devices  38.6 us (33%)
  waiting for transfers between devices  31.2 us (27%)
  local copies, waits for them, and re-layouts  3.35 us (3%)
  other arithmetic  2.54 us (2%)
    pallas_call x1, Pallas kernels, couple(): pl.pallas_call(couple_kernel, out_shape=(half, half, entry, entry), in_sp...  24.3 us
    ppermute x1, waiting for transfers between devices, step(): part_a = part_a + lax.ppermute(part_a, 'xl', ways['xl'])  10.4 us
    pallas_call x1, Pallas kernels, solve(): pl.pallas_call(solve_kernel, out_shape=jax.ShapeDtypeStruct((HALF, COLS),...  10.3 us
    ppermute x1, starting transfers between devices, step(): col_b = lax.ppermute(col_b, BLK, pairs(8, 1))  6.58 us
    ppermute x1, waiting for transfers between devices, step(): far = lax.ppermute(far, 'xh', flip(2, 1))  5.3 us
    ppermute x3, starting transfers between devices, step(): lax.ppermute(packet, 'y', flip(4, k))  4.7 us
    ppermute x1, waiting for transfers between devices, step(): lax.ppermute(got, 'xh', flip(2, 1))  4.34 us
    ppermute x1, starting transfers between devices, step(): part_a = part_a + lax.ppermute(part_a, 'z', around)  4.21 us
  transfers between devices with their start and end apart: 23, of which 11 were waited for; matrix products, arithmetic and copies ran while one was open for 1% of the time, Pallas kernels for 11%

profile of v1, /device:TPU:6, one launch (start us, length us, event | category | flops | bytes accessed | tf_op | source)
XLA Modules:
  0.0 116.6 jit_solution(5569816176467811338)
XLA Ops:
  1.3 2.4 %pack.1 = (f32[2,2048]{1,0:T(2,128)}, f32[16,128]{1,0:T(8,128)}, f32[16,128]{1,0:T(8,128)}, f32[16,64]{1,0:T(8,128)}, f32[16,64]{1,0:T(8,128)}) custom-call(s32[4]{0:T(128)} %pad_add_fusion.where, f32[8,64,128]{2,1,0:T(8,128)} %temp.3, f32[8,64,128]{2,1,0:T(8,128)} %uvel.3, f32[8,64,128]{2,1,0:T(8,128)} %vvel.3, s32[1,1,2048]{2,1,0:T(1,128)} %col.3, ...), custom_call_target="tpu_custom_call" | custom-call | flops 60000000 | tf_op jit(solution)/shard_map/pack/pallas_call | solution.py:93
  3.7 1.6 %collective-permute-start.4 = (f32[2,2048]{1,0:T(2,128)}, f32[2,2048]{1,0:T(2,128)S(1)}, u32[]{:S(2)}, u32[]{:S(2)}) collective-permute-start(f32[2,2048]{1,0:T(2,128)} %get-tuple-element.15.packet), channel_id=1, source_target_pairs={{0,1},{1,0},{2,3},{3,2},{4,5},{5,4},{6,7},{7,6},{8,9},{9,8},{10,11... | collective-permute-start | bytes 49160 | tf_op jit(solution)/shard_map/ppermute | solution.py:541
  5.3 2.9 %collective-permute-start.5 = (f32[2,2048]{1,0:T(2,128)}, f32[2,2048]{1,0:T(2,128)S(1)}, u32[]{:S(2)}, u32[]{:S(2)}) collective-permute-start(f32[2,2048]{1,0:T(2,128)} %get-tuple-element.15.packet), channel_id=1, source_target_pairs={{0,2},{1,3},{2,0},{3,1},{4,6},{5,7},{6,4},{7,5},{8,10},{9,11},{10,... | collective-permute-start | bytes 49160 | tf_op jit(solution)/shard_map/ppermute | solution.py:541
  9.1 1.6 %collective-permute-done.5 = f32[2,2048]{1,0:T(2,128)S(1)} collective-permute-done((f32[2,2048]{1,0:T(2,128)}, f32[2,2048]{1,0:T(2,128)S(1)}, u32[]{:S(2)}, u32[]{:S(2)}) %collective-permute-start.5) | collective-permute-done | bytes 16416 | tf_op jit(solution)/shard_map/ppermute | solution.py:541
  10.7 2.6 %collective-permute-done.6 = f32[2,2048]{1,0:T(2,128)S(1)} collective-permute-done((f32[2,2048]{1,0:T(2,128)}, f32[2,2048]{1,0:T(2,128)S(1)}, u32[]{:S(2)}, u32[]{:S(2)}) %collective-permute-start.6) | collective-permute-done | bytes 16416 | tf_op jit(solution)/shard_map/ppermute | solution.py:541
  14.1 1.5 %collective-permute-start.7 = (f32[4,2,2048]{2,1,0:T(2,128)S(1)}, f32[4,2,2048]{2,1,0:T(2,128)S(1)}, u32[]{:S(2)}, u32[]{:S(2)}) collective-permute-start(f32[4,2,2048]{2,1,0:T(2,128)S(1)} %pad_maximum_fusion.2), channel_id=1, source_target_pairs={{0,4},{4,0},{1,5},{5,1},{2,6},{6,2},{3,7},{7,3},{8,12},{12,8},{9,1... | collective-permute-start | bytes 196616 | tf_op jit(solution)/shard_map/ppermute | solution.py:543
  15.6 4.3 %collective-permute-done.7 = f32[4,2,2048]{2,1,0:T(2,128)S(1)} collective-permute-done((f32[4,2,2048]{2,1,0:T(2,128)S(1)}, f32[4,2,2048]{2,1,0:T(2,128)S(1)}, u32[]{:S(2)}, u32[]{:S(2)}) %collective-permute-start.7) | collective-permute-done | bytes 65568 | tf_op jit(solution)/shard_map/ppermute | solution.py:543
  20.6 24.3 %couple.1 = (f32[64,1024]{1,0:T(8,128)}, f32[64,1024]{1,0:T(8,128)}, f32[4,1,2048]{2,1,0:T(1,128)}, f32[4,1,2048]{2,1,0:T(1,128)}) custom-call(s32[4]{0:T(128)} %pad_add_fusion.where, f32[8,2,2048]{2,1,0:T(2,128)} %copy-done.17, f32[128,1024]{1,0:T(8,128)} %thick.1), custom_call_target="tpu_custom_call" | custom-call | flops 480000000 | tf_op jit(solution)/shard_map/couple/pallas_call | solution.py:184
  45.0 3.1 %collective-permute-start.21 = (f32[3,64,1024]{2,1,0:T(8,128)S(1)}, f32[3,64,1024]{2,1,0:T(8,128)S(1)}, u32[]{:S(2)}, u32[]{:S(2)}) collective-permute-start(f32[3,64,1024]{2,1,0:T(8,128)S(1)} %fusion.1), channel_id=1, source_target_pairs={{1,8},{2,9},{3,10},{4,11},{5,12},{6,13},{7,14},{8,1},{9,2},{10,3},... | collective-permute-start | bytes 2359304 | tf_op jit(solution)/shard_map/ppermute | solution.py:549
  48.2 2.0 %collective-permute-start.16 = (f32[32,1024]{1,0:T(8,128)S(1)}, f32[32,1024]{1,0:T(8,128)S(1)}, u32[]{:S(2)}, u32[]{:S(2)}) collective-permute-start(f32[32,1024]{1,0:T(8,128)S(1)} %get-tuple-element.23), channel_id=1, source_target_pairs={{0,32},{32,0},{64,96},{96,64},{1,33},{33,1},{65,97},{97,65},{2,34}... | collective-permute-start | bytes 393224 | tf_op jit(solution)/shard_map/ppermute | solution.py:563
  50.2 10.4 %collective-permute-done.13 = f32[32,1024]{1,0:T(8,128)S(1)} collective-permute-done((f32[32,1024]{1,0:T(8,128)S(1)}, f32[32,1024]{1,0:T(8,128)S(1)}, u32[]{:S(2)}, u32[]{:S(2)}) %collective-permute-start.13) | collective-permute-done | bytes 131104 | tf_op jit(solution)/shard_map/ppermute | solution.py:562
  60.6 2.1 %collective-permute-start.14 = (f32[32,1024]{1,0:T(8,128)S(1)}, f32[32,1024]{1,0:T(8,128)S(1)}, u32[]{:S(2)}, u32[]{:S(2)}) collective-permute-start(f32[32,1024]{1,0:T(8,128)S(1)} %add.41), channel_id=1, source_target_pairs={{0,32},{32,0},{64,96},{96,64},{1,33},{33,1},{65,97},{97,65},{2,34}... | collective-permute-start | bytes 393224 | tf_op jit(solution)/shard_map/ppermute | solution.py:564
  62.8 2.6 %collective-permute-start.17 = (f32[32,1024]{1,0:T(8,128)S(1)}, f32[32,1024]{1,0:T(8,128)S(1)}, u32[]{:S(2)}, u32[]{:S(2)}) collective-permute-start(f32[32,1024]{1,0:T(8,128)S(1)} %add.45), channel_id=1, source_target_pairs={{0,96},{32,64},{64,32},{96,0},{1,97},{33,65},{65,33},{97,1},{2,98}... | collective-permute-start | bytes 393224 | tf_op jit(solution)/shard_map/ppermute | solution.py:565
  65.7 4.2 %collective-permute-start.15 = (f32[32,1024]{1,0:T(8,128)S(1)}, f32[32,1024]{1,0:T(8,128)S(1)}, u32[]{:S(2)}, u32[]{:S(2)}) collective-permute-start(f32[32,1024]{1,0:T(8,128)S(1)} %add.42), channel_id=1, source_target_pairs={{0,96},{32,64},{64,32},{96,0},{1,97},{33,65},{65,33},{97,1},{2,98}... | collective-permute-start | bytes 393224 | tf_op jit(solution)/shard_map/ppermute | solution.py:568
  70.0 2.0 %collective-permute-start.18 = (f32[32,1024]{1,0:T(8,128)S(1)}, f32[32,1024]{1,0:T(8,128)S(1)}, u32[]{:S(2)}, u32[]{:S(2)}) collective-permute-start(f32[32,1024]{1,0:T(8,128)S(1)} %add.46), channel_id=1, source_target_pairs={{0,16},{16,0},{1,17},{17,1},{2,18},{18,2},{3,19},{19,3},{4,20},{20... | collective-permute-start | bytes 393224 | tf_op jit(solution)/shard_map/ppermute | solution.py:569
  72.9 2.1 %collective-permute-done.18 = f32[32,1024]{1,0:T(8,128)S(1)} collective-permute-done((f32[32,1024]{1,0:T(8,128)S(1)}, f32[32,1024]{1,0:T(8,128)S(1)}, u32[]{:S(2)}, u32[]{:S(2)}) %collective-permute-start.18) | collective-permute-done | bytes 131104 | tf_op jit(solution)/shard_map/ppermute | solution.py:569
  75.2 3.5 %collective-permute-start.20 = (f32[64,1024]{1,0:T(8,128)S(1)}, f32[64,1024]{1,0:T(8,128)S(1)}, u32[]{:S(2)}, u32[]{:S(2)}) collective-permute-start(f32[64,1024]{1,0:T(8,128)S(1)} %pad_maximum_fusion.1.own), channel_id=1, source_target_pairs={{1,8},{2,9},{3,10},{4,11},{5,12},{6,13},{7,14},{8,1},{9,2},{10,3},... | collective-permute-start | bytes 786440 | tf_op jit(solution)/shard_map/ppermute | solution.py:572
  78.9 5.3 %collective-permute-done.8 = f32[4,1,2048]{2,1,0:T(1,128)S(1)} collective-permute-done((f32[4,1,2048]{2,1,0:T(1,128)S(1)}, f32[4,1,2048]{2,1,0:T(1,128)S(1)}, u32[]{:S(2)}, u32[]{:S(2)}) %collective-permute-start.8) | collective-permute-done | bytes 32800 | tf_op jit(solution)/shard_map/ppermute | solution.py:557
  84.2 1.9 %collective-permute-start.1 = (f32[16,128]{1,0:T(8,128)S(1)}, f32[16,128]{1,0:T(8,128)S(1)}, u32[]{:S(2)}, u32[]{:S(2)}) collective-permute-start(f32[16,128]{1,0:T(8,128)S(1)} %copy-done.19), channel_id=1, source_target_pairs={{8,16},{24,32},{40,48},{56,64},{72,80},{88,96},{104,112},{16,8},{3... | collective-permute-start | bytes 24584 | tf_op jit(solution)/shard_map/ppermute | solution.py:551
  86.8 6.6 %collective-permute-start.3 = (f32[16,64]{1,0:T(8,128)S(1)}, f32[16,64]{1,0:T(8,128)S(1)}, u32[]{:S(2)}, u32[]{:S(2)}) collective-permute-start(f32[16,64]{1,0:T(8,128)S(1)} %copy-done.21), channel_id=1, source_target_pairs={{1,2},{3,4},{5,6},{2,1},{4,3},{6,5},{9,10},{11,12},{13,14},{10,9},... | collective-permute-start | bytes 12296 | tf_op jit(solution)/shard_map/ppermute | solution.py:553
  94.2 10.3 %solve.1 = f32[64,1024]{1,0:T(8,128)} custom-call(s32[4]{0:T(128)} %pad_add_fusion.where, f32[64,1024]{1,0:T(8,128)} %copy-done.3, f32[64,1024]{1,0:T(8,128)} %copy-done.6, f32[64,1024]{1,0:T(8,128)} %copy-done.7, f32[128,1024]{1,0:T(8,128)} %visc.1, f32[128,1024]{1,0:T(8,128)} %fric.1, f32[128,1024]{1,0:T(8,128)} %drive.1, f32[3,64,1024]{2,1,0:T(8,128)} %copy-done.5), custom_call_target="tpu_custom_call" | custom-call | flops 200000000 | tf_op jit(solution)/shard_map/solve/pallas_call | solution.py:499
  105.9 2.6 %collective-permute-start.11 = (f32[1,2048]{1,0:T(1,128)S(1)}, f32[1,2048]{1,0:T(1,128)S(1)}, u32[]{:S(2)}, u32[]{:S(2)}) collective-permute-start(f32[1,2048]{1,0:T(1,128)S(1)} %get-tuple-element.24), channel_id=1, source_target_pairs={{0,3},{1,2},{2,1},{3,0},{4,7},{5,6},{6,5},{7,4},{8,11},{9,10},{10,... | collective-permute-start | bytes 24584 | tf_op jit(solution)/shard_map/ppermute | solution.py:567
  108.6 1.6 %collective-permute-done.10 = f32[1,2048]{1,0:T(1,128)S(1)} collective-permute-done((f32[1,2048]{1,0:T(1,128)S(1)}, f32[1,2048]{1,0:T(1,128)S(1)}, u32[]{:S(2)}, u32[]{:S(2)}) %collective-permute-start.10) | collective-permute-done | bytes 8224 | tf_op jit(solution)/shard_map/ppermute | solution.py:567
  112.8 2.8 %ocean.1 = f32[8,64,128]{2,1,0:T(8,128)} custom-call(s32[4]{0:T(128)} %pad_add_fusion.where, f32[8,64,128]{2,1,0:T(8,128)} %temp.3, f32[8,64,128]{2,1,0:T(8,128)} %uvel.3, f32[8,64,128]{2,1,0:T(8,128)} %vvel.3, f32[16,128]{1,0:T(8,128)} %copy-done.10, f32[16,128]{1,0:T(8,128)} %copy-done.11, f32[16,64]{1,0:T(8,128)} %copy-done.12, f32[16,64]{1,0:T(8,128)} %copy-done.13, ...), custom_call_target="tpu_custom_call" | custom-call | flops 60000000 | tf_op jit(solution)/shard_map/ocean/pallas_call | solution.py:262
  (92 shorter events, 11.1 us)
Async XLA Ops:
  3.7 5.5 %collective-permute-start.4 = (f32[2,2048]{1,0:T(2,128)}, f32[2,2048]{1,0:T(2,128)S(1)}, u32[]{:S(2)}, u32[]{:S(2)}) collective-permute-start(f32[2,2048]{1,0:T(2,128)} %get-tuple-element.15.packet), channel_id=1, source_target_pairs={{0,1},{1,0},{2,3},{3,2},{4,5},{5,4},{6,7},{7,6},{8,9},{9,8},{10,11... | collective-permute-start | bytes 49160 | tf_op jit(solution)/shard_map/ppermute | solution.py:541
  5.3 5.5 %collective-permute-start.5 = (f32[2,2048]{1,0:T(2,128)}, f32[2,2048]{1,0:T(2,128)S(1)}, u32[]{:S(2)}, u32[]{:S(2)}) collective-permute-start(f32[2,2048]{1,0:T(2,128)} %get-tuple-element.15.packet), channel_id=1, source_target_pairs={{0,2},{1,3},{2,0},{3,1},{4,6},{5,7},{6,4},{7,5},{8,10},{9,11},{10,... | collective-permute-start | bytes 49160 | tf_op jit(solution)/shard_map/ppermute | solution.py:541
  8.2 5.2 %collective-permute-start.6 = (f32[2,2048]{1,0:T(2,128)}, f32[2,2048]{1,0:T(2,128)S(1)}, u32[]{:S(2)}, u32[]{:S(2)}) collective-permute-start(f32[2,2048]{1,0:T(2,128)} %get-tuple-element.15.packet), channel_id=1, source_target_pairs={{0,3},{1,2},{2,1},{3,0},{4,7},{5,6},{6,5},{7,4},{8,11},{9,10},{10,... | collective-permute-start | bytes 49160 | tf_op jit(solution)/shard_map/ppermute | solution.py:541
  14.1 5.8 %collective-permute-start.7 = (f32[4,2,2048]{2,1,0:T(2,128)S(1)}, f32[4,2,2048]{2,1,0:T(2,128)S(1)}, u32[]{:S(2)}, u32[]{:S(2)}) collective-permute-start(f32[4,2,2048]{2,1,0:T(2,128)S(1)} %pad_maximum_fusion.2), channel_id=1, source_target_pairs={{0,4},{4,0},{1,5},{5,1},{2,6},{6,2},{3,7},{7,3},{8,12},{12,8},{9,1... | collective-permute-start | bytes 196616 | tf_op jit(solution)/shard_map/ppermute | solution.py:543
  20.6 24.3 %copy-start.2 = (f32[128,1024]{1,0:T(8,128)S(1)}, f32[128,1024]{1,0:T(8,128)}, u32[]{:S(2)}) copy-start(f32[128,1024]{1,0:T(8,128)} %drive.1) | copy-start | bytes 1572868
  44.8 3.2 %collective-permute-start.12 = (f32[64,1024]{1,0:T(8,128)}, f32[64,1024]{1,0:T(8,128)S(1)}, u32[]{:S(2)}, u32[]{:S(2)}) collective-permute-start(f32[64,1024]{1,0:T(8,128)} %get-tuple-element.19), channel_id=1, source_target_pairs={{0,8},{8,0},{1,9},{9,1},{2,10},{10,2},{3,11},{11,3},{4,12},{12,4},... | collective-permute-start | bytes 786440 | tf_op jit(solution)/shard_map/ppermute | solution.py:556
  45.0 41.2 %collective-permute-start.21 = (f32[3,64,1024]{2,1,0:T(8,128)S(1)}, f32[3,64,1024]{2,1,0:T(8,128)S(1)}, u32[]{:S(2)}, u32[]{:S(2)}) collective-permute-start(f32[3,64,1024]{2,1,0:T(8,128)S(1)} %fusion.1), channel_id=1, source_target_pairs={{1,8},{2,9},{3,10},{4,11},{5,12},{6,13},{7,14},{8,1},{9,2},{10,3},... | collective-permute-start | bytes 2359304 | tf_op jit(solution)/shard_map/ppermute | solution.py:549
  48.1 12.5 %collective-permute-start.13 = (f32[32,1024]{1,0:T(8,128)S(1)}, f32[32,1024]{1,0:T(8,128)S(1)}, u32[]{:S(2)}, u32[]{:S(2)}) collective-permute-start(f32[32,1024]{1,0:T(8,128)S(1)} %get-tuple-element.22), channel_id=1, source_target_pairs={{0,16},{16,0},{1,17},{17,1},{2,18},{18,2},{3,19},{19,3},{4,20},{20... | collective-permute-start | bytes 393224 | tf_op jit(solution)/shard_map/ppermute | solution.py:562
  48.2 14.6 %collective-permute-start.16 = (f32[32,1024]{1,0:T(8,128)S(1)}, f32[32,1024]{1,0:T(8,128)S(1)}, u32[]{:S(2)}, u32[]{:S(2)}) collective-permute-start(f32[32,1024]{1,0:T(8,128)S(1)} %get-tuple-element.23), channel_id=1, source_target_pairs={{0,32},{32,0},{64,96},{96,64},{1,33},{33,1},{65,97},{97,65},{2,34}... | collective-permute-start | bytes 393224 | tf_op jit(solution)/shard_map/ppermute | solution.py:563
  60.6 5.1 %collective-permute-start.14 = (f32[32,1024]{1,0:T(8,128)S(1)}, f32[32,1024]{1,0:T(8,128)S(1)}, u32[]{:S(2)}, u32[]{:S(2)}) collective-permute-start(f32[32,1024]{1,0:T(8,128)S(1)} %add.41), channel_id=1, source_target_pairs={{0,32},{32,0},{64,96},{96,64},{1,33},{33,1},{65,97},{97,65},{2,34}... | collective-permute-start | bytes 393224 | tf_op jit(solution)/shard_map/ppermute | solution.py:564
  62.8 7.2 %collective-permute-start.17 = (f32[32,1024]{1,0:T(8,128)S(1)}, f32[32,1024]{1,0:T(8,128)S(1)}, u32[]{:S(2)}, u32[]{:S(2)}) collective-permute-start(f32[32,1024]{1,0:T(8,128)S(1)} %add.45), channel_id=1, source_target_pairs={{0,96},{32,64},{64,32},{96,0},{1,97},{33,65},{65,33},{97,1},{2,98}... | collective-permute-start | bytes 393224 | tf_op jit(solution)/shard_map/ppermute | solution.py:565
  65.7 7.2 %collective-permute-start.15 = (f32[32,1024]{1,0:T(8,128)S(1)}, f32[32,1024]{1,0:T(8,128)S(1)}, u32[]{:S(2)}, u32[]{:S(2)}) collective-permute-start(f32[32,1024]{1,0:T(8,128)S(1)} %add.42), channel_id=1, source_target_pairs={{0,96},{32,64},{64,32},{96,0},{1,97},{33,65},{65,33},{97,1},{2,98}... | collective-permute-start | bytes 393224 | tf_op jit(solution)/shard_map/ppermute | solution.py:568
  70.0 5.0 %collective-permute-start.18 = (f32[32,1024]{1,0:T(8,128)S(1)}, f32[32,1024]{1,0:T(8,128)S(1)}, u32[]{:S(2)}, u32[]{:S(2)}) collective-permute-start(f32[32,1024]{1,0:T(8,128)S(1)} %add.46), channel_id=1, source_target_pairs={{0,16},{16,0},{1,17},{17,1},{2,18},{18,2},{3,19},{19,3},{4,20},{20... | collective-permute-start | bytes 393224 | tf_op jit(solution)/shard_map/ppermute | solution.py:569
  75.1 11.7 %collective-permute-start.19 = (f32[64,1024]{1,0:T(8,128)S(1)}, f32[64,1024]{1,0:T(8,128)S(1)}, u32[]{:S(2)}, u32[]{:S(2)}) collective-permute-start(f32[64,1024]{1,0:T(8,128)S(1)} %pad_maximum_fusion.1.own), channel_id=1, source_target_pairs={{0,8},{8,0},{1,9},{9,1},{2,10},{10,2},{3,11},{11,3},{4,12},{12,4},... | collective-permute-start | bytes 786440 | tf_op jit(solution)/shard_map/ppermute | solution.py:571
  75.2 18.2 %collective-permute-start.20 = (f32[64,1024]{1,0:T(8,128)S(1)}, f32[64,1024]{1,0:T(8,128)S(1)}, u32[]{:S(2)}, u32[]{:S(2)}) collective-permute-start(f32[64,1024]{1,0:T(8,128)S(1)} %pad_maximum_fusion.1.own), channel_id=1, source_target_pairs={{1,8},{2,9},{3,10},{4,11},{5,12},{6,13},{7,14},{8,1},{9,2},{10,3},... | collective-permute-start | bytes 786440 | tf_op jit(solution)/shard_map/ppermute | solution.py:572
  78.7 5.5 %collective-permute-start.8 = (f32[4,1,2048]{2,1,0:T(1,128)S(1)}, f32[4,1,2048]{2,1,0:T(1,128)S(1)}, u32[]{:S(2)}, u32[]{:S(2)}) collective-permute-start(f32[4,1,2048]{2,1,0:T(1,128)S(1)} %copy-done.18), channel_id=1, source_target_pairs={{0,4},{4,0},{1,5},{5,1},{2,6},{6,2},{3,7},{7,3},{8,12},{12,8},{9,1... | collective-permute-start | bytes 98312 | tf_op jit(solution)/shard_map/ppermute | solution.py:557
  78.8 29.7 %collective-permute-start = (f32[16,128]{1,0:T(8,128)S(1)}, f32[16,128]{1,0:T(8,128)S(1)}, u32[]{:S(2)}, u32[]{:S(2)}) collective-permute-start(f32[16,128]{1,0:T(8,128)S(1)} %copy-done.20), channel_id=1, source_target_pairs={{0,8},{8,0},{1,9},{9,1},{2,10},{10,2},{3,11},{11,3},{4,12},{12,4},... | collective-permute-start | bytes 24584 | tf_op jit(solution)/shard_map/ppermute | solution.py:550
  84.2 24.4 %collective-permute-start.1 = (f32[16,128]{1,0:T(8,128)S(1)}, f32[16,128]{1,0:T(8,128)S(1)}, u32[]{:S(2)}, u32[]{:S(2)}) collective-permute-start(f32[16,128]{1,0:T(8,128)S(1)} %copy-done.19), channel_id=1, source_target_pairs={{8,16},{24,32},{40,48},{56,64},{72,80},{88,96},{104,112},{16,8},{3... | collective-permute-start | bytes 24584 | tf_op jit(solution)/shard_map/ppermute | solution.py:551
  86.2 18.9 %collective-permute-start.2 = (f32[16,64]{1,0:T(8,128)S(1)}, f32[16,64]{1,0:T(8,128)S(1)}, u32[]{:S(2)}, u32[]{:S(2)}) collective-permute-start(f32[16,64]{1,0:T(8,128)S(1)} %copy-done.22), channel_id=1, source_target_pairs={{0,1},{1,0},{2,3},{3,2},{4,5},{5,4},{6,7},{7,6},{8,9},{9,8},{10,11... | collective-permute-start | bytes 12296 | tf_op jit(solution)/shard_map/ppermute | solution.py:552
  86.8 19.1 %collective-permute-start.3 = (f32[16,64]{1,0:T(8,128)S(1)}, f32[16,64]{1,0:T(8,128)S(1)}, u32[]{:S(2)}, u32[]{:S(2)}) collective-permute-start(f32[16,64]{1,0:T(8,128)S(1)} %copy-done.21), channel_id=1, source_target_pairs={{1,2},{3,4},{5,6},{2,1},{4,3},{6,5},{9,10},{11,12},{13,14},{10,9},... | collective-permute-start | bytes 12296 | tf_op jit(solution)/shard_map/ppermute | solution.py:553
  104.5 11.2 %collective-permute-start.22 = (f32[64,1024]{1,0:T(8,128)}, f32[64,1024]{1,0:T(8,128)S(1)}, u32[]{:S(2)}, u32[]{:S(2)}) collective-permute-start(f32[64,1024]{1,0:T(8,128)} %solve.1), channel_id=1, source_target_pairs={{0,8},{8,0},{1,9},{9,1},{2,10},{10,2},{3,11},{11,3},{4,12},{12,4},... | collective-permute-start | bytes 786440 | tf_op jit(solution)/shard_map/ppermute | solution.py:574
  105.1 5.2 %collective-permute-start.10 = (f32[1,2048]{1,0:T(1,128)S(1)}, f32[1,2048]{1,0:T(1,128)S(1)}, u32[]{:S(2)}, u32[]{:S(2)}) collective-permute-start(f32[1,2048]{1,0:T(1,128)S(1)} %get-tuple-element.25), channel_id=1, source_target_pairs={{0,2},{1,3},{2,0},{3,1},{4,6},{5,7},{6,4},{7,5},{8,10},{9,11},{10,... | collective-permute-start | bytes 24584 | tf_op jit(solution)/shard_map/ppermute | solution.py:567
  105.9 4.9 %collective-permute-start.11 = (f32[1,2048]{1,0:T(1,128)S(1)}, f32[1,2048]{1,0:T(1,128)S(1)}, u32[]{:S(2)}, u32[]{:S(2)}) collective-permute-start(f32[1,2048]{1,0:T(1,128)S(1)} %get-tuple-element.24), channel_id=1, source_target_pairs={{0,3},{1,2},{2,1},{3,0},{4,7},{5,6},{6,5},{7,4},{8,11},{9,10},{10,... | collective-permute-start | bytes 24584 | tf_op jit(solution)/shard_map/ppermute | solution.py:567
  108.6 3.7 %collective-permute-start.9 = (f32[1,2048]{1,0:T(1,128)S(1)}, f32[1,2048]{1,0:T(1,128)S(1)}, u32[]{:S(2)}, u32[]{:S(2)}) collective-permute-start(f32[1,2048]{1,0:T(1,128)S(1)} %get-tuple-element.26), channel_id=1, source_target_pairs={{0,1},{1,0},{2,3},{3,2},{4,5},{5,4},{6,7},{7,6},{8,9},{9,8},{10,11... | collective-permute-start | bytes 24584 | tf_op jit(solution)/shard_map/ppermute | solution.py:567
  (22 other events, 219.3 us)

commit v2 on v1

--- a/solution.py
+++ b/solution.py
@@ -25,7 +25,7 @@
 HALF = 64
 ENT = 2048
 EXT = 192
-KC = 512
+KC = 1024
 CELLS = ROWS * COLS
 f32 = jnp.float32
 bf16 = jnp.bfloat16
@@ -108,7 +108,7 @@
 
 def place(packets, first, k):
     at = pl.multiple_of((k % (ENT // KC)) * KC, KC)
-    index = packets[k // (ENT // KC), 0:1, pl.ds(at, KC)].astype(i32)
+    index = packets[k // (ENT // KC) % 4, 0:1, pl.ds(at, KC)].astype(i32)
     local = index - first
     row = local >> 10
     spot = ((row >> 3) << 6) | (((local >> 7) & 7) << 3) | (row & 7)
@@ -116,7 +116,7 @@
     return spot, local & 127, at
 
 
-def couple_kernel(where, packets, thick, mine, other, near, far, tiles, table, onehot, lanes, acc, melt):
+def couple_kernel(where, close, away, thick, mine, other, near, far, tiles, table, onehot, lanes, acc, melt):
     first, core = where[0], where[1]
     acc[...] = jnp.zeros_like(acc)
     for t in range(128):
@@ -127,7 +127,7 @@
         table[0:128, a * 128 : a * 128 + 128] = high
         table[128:256, a * 128 : a * 128 + 128] = low
 
-    def fetch(k, p, out):
+    def fetch(k, p, packets, out):
         spot, lane, at = place(packets, first, k)
         onehot[p] = jnp.where(lax.broadcasted_iota(jnp.int16, (1024, KC), 0) == spot.astype(jnp.int16), jnp.array(1.0, bf16), jnp.array(0.0, bf16))
         picked = jnp.dot(table[...], onehot[p], preferred_element_type=f32)
@@ -136,7 +136,7 @@
         draft = jnp.sum(jnp.where(mask, picked, 0.0), axis=0, keepdims=True)
         s = k // (ENT // KC)
         out[s % 4, 0:1, pl.ds(at, KC)] = draft
-        value = melt_rate * (packets[s, 1:2, pl.ds(at, KC)] + 0.5 + 0.5 * draft)
+        value = melt_rate * (packets[s % 4, 1:2, pl.ds(at, KC)] + 0.5 + 0.5 * draft)
         high, low = split2(value)
         mask = lax.broadcasted_iota(jnp.int16, (128, KC), 0) == lane.astype(jnp.int16)
         zero = jnp.array(0.0, bf16)
@@ -149,16 +149,16 @@
     per = 4 * ENT // KC
 
     def near_chunk(h, carry):
-        fetch(2 * h, 0, near)
+        fetch(2 * h, 0, close, near)
         spread(1)
-        fetch(2 * h + 1, 1, near)
+        fetch(2 * h + 1, 1, close, near)
         spread(0)
         return carry
 
     def far_chunk(h, carry):
-        fetch(2 * h, 0, far)
+        fetch(2 * h, 0, away, far)
         spread(1)
-        fetch(2 * h + 1, 1, far)
+        fetch(2 * h + 1, 1, away, far)
         spread(0)
         return carry
 
@@ -178,13 +178,13 @@
     other[...] = melt[1 - core]
 
 
-def couple(where, packets, thick):
+def couple(where, close, away, thick):
     half = jax.ShapeDtypeStruct((HALF, COLS), f32)
     entry = jax.ShapeDtypeStruct((4, 1, ENT), f32)
     return pl.pallas_call(
         couple_kernel,
         out_shape=(half, half, entry, entry),
-        in_specs=[SMEM, VMEM, VMEM],
+        in_specs=[SMEM, VMEM, VMEM, VMEM],
         out_specs=(VMEM,) * 4,
         scratch_shapes=[
             pltpu.VMEM((1024, 128), f32),
@@ -196,7 +196,7 @@
         ],
         cost_estimate=cost(24),
         name="couple",
-    )(where, packets, thick)
+    )(where, close, away, thick)
 
 
 def ocean_kernel(
@@ -540,7 +540,7 @@
     packet, row_a, row_b, col_a, col_b = pack(where, temp, uvel, vvel, col, cell, cav)
     got = [packet] + [lax.ppermute(packet, "y", flip(4, k)) for k in range(1, 4)]
     got = jnp.stack(got)
-    packets = jnp.concatenate([got, lax.ppermute(got, "xh", flip(2, 1))], axis=0)
+    away = lax.ppermute(got, "xh", flip(2, 1))
 
     ring = ("co", "xh", "y")
     outer = [(b, 8 + b - 1) for b in range(1, 8)] + [(8 + b, b + 1) for b in range(7)]
@@ -552,7 +552,7 @@
     col_a = lax.ppermute(col_a, "y", flip(4, 1))
     col_b = lax.ppermute(col_b, BLK, pairs(8, 1))
 
-    mine, other, close, far = couple(where, packets, thick)
+    mine, other, close, far = couple(where, got, away, thick)
     theirs = lax.ppermute(other, "co", flip(2, 1))
     far = lax.ppermute(far, "xh", flip(2, 1))
     part_a = mine[:32] + theirs[:32]

time: 117 us -> 116 us (level)
  Pallas kernels: 39.8 us -> 38.6 us
    pallas_call x1, Pallas kernels: 24.3 us -> 23.1 us  [couple(): pl.pallas_call(couple_kernel, out_shape=(half, half, entry, entry), in_sp...]
    unnamed x50 -> x48, local copies, waits for them, and re-layouts: 2.74 us -> 1.96 us
where the time goes in v2:
time: 116 us; the launch traced here: 115 us
  Pallas kernels  38.6 us (33%)
  starting transfers between devices  38.6 us (33%)
  waiting for transfers between devices  32 us (28%)
  local copies, waits for them, and re-layouts  2.56 us (2%)
  other arithmetic  2.5 us (2%)
    pallas_call x1, Pallas kernels, couple(): pl.pallas_call(couple_kernel, out_shape=(half, half, entry, entry), in_sp...  23.1 us
    ppermute x1, waiting for transfers between devices, step(): part_a = part_a + lax.ppermute(part_a, 'xl', ways['xl'])  10.4 us
    pallas_call x1, Pallas kernels, solve(): pl.pallas_call(solve_kernel, out_shape=jax.ShapeDtypeStruct((HALF, COLS),...  10.3 us
    ppermute x1, starting transfers between devices, step(): col_b = lax.ppermute(col_b, BLK, pairs(8, 1))  6.58 us
    ppermute x1, waiting for transfers between devices, step(): far = lax.ppermute(far, 'xh', flip(2, 1))  5.3 us
    ppermute x3, waiting for transfers between devices, step(): lax.ppermute(packet, 'y', flip(4, k))  4.94 us
    ppermute x3, starting transfers between devices, step(): lax.ppermute(packet, 'y', flip(4, k))  4.7 us
    ppermute x1, waiting for transfers between devices, step(): away = lax.ppermute(got, 'xh', flip(2, 1))  4.36 us
  transfers between devices with their start and end apart: 23, of which 11 were waited for; matrix products, arithmetic and copies ran while one was open for 1% of the time, Pallas kernels for 11%

profile of v2, /device:TPU:6, one launch (start us, length us, event | category | flops | bytes accessed | tf_op | source)
XLA Modules:
  0.0 115.4 jit_solution(7001345084612586733)
XLA Ops:
  1.2 2.4 %pack.1 = (f32[2,2048]{1,0:T(2,128)}, f32[16,128]{1,0:T(8,128)}, f32[16,128]{1,0:T(8,128)}, f32[16,64]{1,0:T(8,128)}, f32[16,64]{1,0:T(8,128)}) custom-call(s32[4]{0:T(128)} %pad_add_fusion.where, f32[8,64,128]{2,1,0:T(8,128)} %temp.3, f32[8,64,128]{2,1,0:T(8,128)} %uvel.3, f32[8,64,128]{2,1,0:T(8,128)} %vvel.3, s32[1,1,2048]{2,1,0:T(1,128)} %col.3, ...), custom_call_target="tpu_custom_call" | custom-call | flops 60000000 | tf_op jit(solution)/shard_map/pack/pallas_call | solution.py:93
  3.6 1.6 %collective-permute-start.4 = (f32[2,2048]{1,0:T(2,128)}, f32[2,2048]{1,0:T(2,128)S(1)}, u32[]{:S(2)}, u32[]{:S(2)}) collective-permute-start(f32[2,2048]{1,0:T(2,128)} %get-tuple-element.15.packet), channel_id=1, source_target_pairs={{0,1},{1,0},{2,3},{3,2},{4,5},{5,4},{6,7},{7,6},{8,9},{9,8},{10,11... | collective-permute-start | bytes 49160 | tf_op jit(solution)/shard_map/ppermute | solution.py:541
  5.2 2.9 %collective-permute-start.5 = (f32[2,2048]{1,0:T(2,128)}, f32[2,2048]{1,0:T(2,128)S(1)}, u32[]{:S(2)}, u32[]{:S(2)}) collective-permute-start(f32[2,2048]{1,0:T(2,128)} %get-tuple-element.15.packet), channel_id=1, source_target_pairs={{0,2},{1,3},{2,0},{3,1},{4,6},{5,7},{6,4},{7,5},{8,10},{9,11},{10,... | collective-permute-start | bytes 49160 | tf_op jit(solution)/shard_map/ppermute | solution.py:541
  8.3 2.3 %collective-permute-done.5 = f32[2,2048]{1,0:T(2,128)S(1)} collective-permute-done((f32[2,2048]{1,0:T(2,128)}, f32[2,2048]{1,0:T(2,128)S(1)}, u32[]{:S(2)}, u32[]{:S(2)}) %collective-permute-start.5) | collective-permute-done | bytes 16416 | tf_op jit(solution)/shard_map/ppermute | solution.py:541
  10.7 2.6 %collective-permute-done.6 = f32[2,2048]{1,0:T(2,128)S(1)} collective-permute-done((f32[2,2048]{1,0:T(2,128)}, f32[2,2048]{1,0:T(2,128)S(1)}, u32[]{:S(2)}, u32[]{:S(2)}) %collective-permute-start.6) | collective-permute-done | bytes 16416 | tf_op jit(solution)/shard_map/ppermute | solution.py:541
  14.1 1.5 %collective-permute-start.7 = (f32[4,2,2048]{2,1,0:T(2,128)S(1)}, f32[4,2,2048]{2,1,0:T(2,128)S(1)}, u32[]{:S(2)}, u32[]{:S(2)}) collective-permute-start(f32[4,2,2048]{2,1,0:T(2,128)S(1)} %pad_maximum_fusion.2.close), channel_id=1, source_target_pairs={{0,4},{4,0},{1,5},{5,1},{2,6},{6,2},{3,7},{7,3},{8,12},{12,8},{9,1... | collective-permute-start | bytes 196616 | tf_op jit(solution)/shard_map/ppermute | solution.py:543
  15.5 4.4 %collective-permute-done.7.away = f32[4,2,2048]{2,1,0:T(2,128)S(1)} collective-permute-done((f32[4,2,2048]{2,1,0:T(2,128)S(1)}, f32[4,2,2048]{2,1,0:T(2,128)S(1)}, u32[]{:S(2)}, u32[]{:S(2)}) %collective-permute-start.7) | collective-permute-done | bytes 65568 | tf_op jit(solution)/shard_map/ppermute | solution.py:543
  20.5 23.1 %couple.1 = (f32[64,1024]{1,0:T(8,128)}, f32[64,1024]{1,0:T(8,128)}, f32[4,1,2048]{2,1,0:T(1,128)}, f32[4,1,2048]{2,1,0:T(1,128)}) custom-call(s32[4]{0:T(128)} %pad_add_fusion.where, f32[4,2,2048]{2,1,0:T(2,128)} %copy-done.9, f32[4,2,2048]{2,1,0:T(2,128)} %copy-done.18, f32[128,1024]{1,0:T(8,128)} %thick.1), custom_call_target="tpu_custom_call" | custom-call | flops 480000000 | tf_op jit(solution)/shard_map/couple/pallas_call | solution.py:184
  43.7 3.1 %collective-permute-start.21 = (f32[3,64,1024]{2,1,0:T(8,128)S(1)}, f32[3,64,1024]{2,1,0:T(8,128)S(1)}, u32[]{:S(2)}, u32[]{:S(2)}) collective-permute-start(f32[3,64,1024]{2,1,0:T(8,128)S(1)} %fusion.1), channel_id=1, source_target_pairs={{1,8},{2,9},{3,10},{4,11},{5,12},{6,13},{7,14},{8,1},{9,2},{10,3},... | collective-permute-start | bytes 2359304 | tf_op jit(solution)/shard_map/ppermute | solution.py:549
  47.0 2.0 %collective-permute-start.16 = (f32[32,1024]{1,0:T(8,128)S(1)}, f32[32,1024]{1,0:T(8,128)S(1)}, u32[]{:S(2)}, u32[]{:S(2)}) collective-permute-start(f32[32,1024]{1,0:T(8,128)S(1)} %get-tuple-element.23), channel_id=1, source_target_pairs={{0,32},{32,0},{64,96},{96,64},{1,33},{33,1},{65,97},{97,65},{2,34}... | collective-permute-start | bytes 393224 | tf_op jit(solution)/shard_map/ppermute | solution.py:563
  49.0 10.4 %collective-permute-done.13 = f32[32,1024]{1,0:T(8,128)S(1)} collective-permute-done((f32[32,1024]{1,0:T(8,128)S(1)}, f32[32,1024]{1,0:T(8,128)S(1)}, u32[]{:S(2)}, u32[]{:S(2)}) %collective-permute-start.13) | collective-permute-done | bytes 131104 | tf_op jit(solution)/shard_map/ppermute | solution.py:562
  59.4 2.1 %collective-permute-start.14 = (f32[32,1024]{1,0:T(8,128)S(1)}, f32[32,1024]{1,0:T(8,128)S(1)}, u32[]{:S(2)}, u32[]{:S(2)}) collective-permute-start(f32[32,1024]{1,0:T(8,128)S(1)} %add.41), channel_id=1, source_target_pairs={{0,32},{32,0},{64,96},{96,64},{1,33},{33,1},{65,97},{97,65},{2,34}... | collective-permute-start | bytes 393224 | tf_op jit(solution)/shard_map/ppermute | solution.py:564
  61.5 2.6 %collective-permute-start.17 = (f32[32,1024]{1,0:T(8,128)S(1)}, f32[32,1024]{1,0:T(8,128)S(1)}, u32[]{:S(2)}, u32[]{:S(2)}) collective-permute-start(f32[32,1024]{1,0:T(8,128)S(1)} %add.45), channel_id=1, source_target_pairs={{0,96},{32,64},{64,32},{96,0},{1,97},{33,65},{65,33},{97,1},{2,98}... | collective-permute-start | bytes 393224 | tf_op jit(solution)/shard_map/ppermute | solution.py:565
  64.5 4.2 %collective-permute-start.15 = (f32[32,1024]{1,0:T(8,128)S(1)}, f32[32,1024]{1,0:T(8,128)S(1)}, u32[]{:S(2)}, u32[]{:S(2)}) collective-permute-start(f32[32,1024]{1,0:T(8,128)S(1)} %add.42), channel_id=1, source_target_pairs={{0,96},{32,64},{64,32},{96,0},{1,97},{33,65},{65,33},{97,1},{2,98}... | collective-permute-start | bytes 393224 | tf_op jit(solution)/shard_map/ppermute | solution.py:568
  68.8 2.0 %collective-permute-start.18 = (f32[32,1024]{1,0:T(8,128)S(1)}, f32[32,1024]{1,0:T(8,128)S(1)}, u32[]{:S(2)}, u32[]{:S(2)}) collective-permute-start(f32[32,1024]{1,0:T(8,128)S(1)} %add.46), channel_id=1, source_target_pairs={{0,16},{16,0},{1,17},{17,1},{2,18},{18,2},{3,19},{19,3},{4,20},{20... | collective-permute-start | bytes 393224 | tf_op jit(solution)/shard_map/ppermute | solution.py:569
  71.7 2.1 %collective-permute-done.18 = f32[32,1024]{1,0:T(8,128)S(1)} collective-permute-done((f32[32,1024]{1,0:T(8,128)S(1)}, f32[32,1024]{1,0:T(8,128)S(1)}, u32[]{:S(2)}, u32[]{:S(2)}) %collective-permute-start.18) | collective-permute-done | bytes 131104 | tf_op jit(solution)/shard_map/ppermute | solution.py:569
  74.0 3.5 %collective-permute-start.20 = (f32[64,1024]{1,0:T(8,128)S(1)}, f32[64,1024]{1,0:T(8,128)S(1)}, u32[]{:S(2)}, u32[]{:S(2)}) collective-permute-start(f32[64,1024]{1,0:T(8,128)S(1)} %pad_maximum_fusion.1.own), channel_id=1, source_target_pairs={{1,8},{2,9},{3,10},{4,11},{5,12},{6,13},{7,14},{8,1},{9,2},{10,3},... | collective-permute-start | bytes 786440 | tf_op jit(solution)/shard_map/ppermute | solution.py:572
  77.7 5.3 %collective-permute-done.8 = f32[4,1,2048]{2,1,0:T(1,128)S(1)} collective-permute-done((f32[4,1,2048]{2,1,0:T(1,128)S(1)}, f32[4,1,2048]{2,1,0:T(1,128)S(1)}, u32[]{:S(2)}, u32[]{:S(2)}) %collective-permute-start.8) | collective-permute-done | bytes 32800 | tf_op jit(solution)/shard_map/ppermute | solution.py:557
  83.0 1.9 %collective-permute-start.1 = (f32[16,128]{1,0:T(8,128)S(1)}, f32[16,128]{1,0:T(8,128)S(1)}, u32[]{:S(2)}, u32[]{:S(2)}) collective-permute-start(f32[16,128]{1,0:T(8,128)S(1)} %copy-done.20), channel_id=1, source_target_pairs={{8,16},{24,32},{40,48},{56,64},{72,80},{88,96},{104,112},{16,8},{3... | collective-permute-start | bytes 24584 | tf_op jit(solution)/shard_map/ppermute | solution.py:551
  85.6 6.6 %collective-permute-start.3 = (f32[16,64]{1,0:T(8,128)S(1)}, f32[16,64]{1,0:T(8,128)S(1)}, u32[]{:S(2)}, u32[]{:S(2)}) collective-permute-start(f32[16,64]{1,0:T(8,128)S(1)} %copy-done.22), channel_id=1, source_target_pairs={{1,2},{3,4},{5,6},{2,1},{4,3},{6,5},{9,10},{11,12},{13,14},{10,9},... | collective-permute-start | bytes 12296 | tf_op jit(solution)/shard_map/ppermute | solution.py:553
  92.9 10.3 %solve.1 = f32[64,1024]{1,0:T(8,128)} custom-call(s32[4]{0:T(128)} %pad_add_fusion.where, f32[64,1024]{1,0:T(8,128)} %copy-done.3, f32[64,1024]{1,0:T(8,128)} %copy-done.6, f32[64,1024]{1,0:T(8,128)} %copy-done.7, f32[128,1024]{1,0:T(8,128)} %visc.1, f32[128,1024]{1,0:T(8,128)} %fric.1, f32[128,1024]{1,0:T(8,128)} %drive.1, f32[3,64,1024]{2,1,0:T(8,128)} %copy-done.5), custom_call_target="tpu_custom_call" | custom-call | flops 200000000 | tf_op jit(solution)/shard_map/solve/pallas_call | solution.py:499
  104.7 2.6 %collective-permute-start.11 = (f32[1,2048]{1,0:T(1,128)S(1)}, f32[1,2048]{1,0:T(1,128)S(1)}, u32[]{:S(2)}, u32[]{:S(2)}) collective-permute-start(f32[1,2048]{1,0:T(1,128)S(1)} %get-tuple-element.24), channel_id=1, source_target_pairs={{0,3},{1,2},{2,1},{3,0},{4,7},{5,6},{6,5},{7,4},{8,11},{9,10},{10,... | collective-permute-start | bytes 24584 | tf_op jit(solution)/shard_map/ppermute | solution.py:567
  107.4 1.6 %collective-permute-done.10 = f32[1,2048]{1,0:T(1,128)S(1)} collective-permute-done((f32[1,2048]{1,0:T(1,128)S(1)}, f32[1,2048]{1,0:T(1,128)S(1)}, u32[]{:S(2)}, u32[]{:S(2)}) %collective-permute-start.10) | collective-permute-done | bytes 8224 | tf_op jit(solution)/shard_map/ppermute | solution.py:567
  111.6 2.8 %ocean.1 = f32[8,64,128]{2,1,0:T(8,128)} custom-call(s32[4]{0:T(128)} %pad_add_fusion.where, f32[8,64,128]{2,1,0:T(8,128)} %temp.3, f32[8,64,128]{2,1,0:T(8,128)} %uvel.3, f32[8,64,128]{2,1,0:T(8,128)} %vvel.3, f32[16,128]{1,0:T(8,128)} %copy-done.11, f32[16,128]{1,0:T(8,128)} %copy-done.12, f32[16,64]{1,0:T(8,128)} %copy-done.13, f32[16,64]{1,0:T(8,128)} %copy-done.14, ...), custom_call_target="tpu_custom_call" | custom-call | flops 60000000 | tf_op jit(solution)/shard_map/ocean/pallas_call | solution.py:262
  (89 shorter events, 10.3 us)
Async XLA Ops:
  3.6 4.7 %collective-permute-start.4 = (f32[2,2048]{1,0:T(2,128)}, f32[2,2048]{1,0:T(2,128)S(1)}, u32[]{:S(2)}, u32[]{:S(2)}) collective-permute-start(f32[2,2048]{1,0:T(2,128)} %get-tuple-element.15.packet), channel_id=1, source_target_pairs={{0,1},{1,0},{2,3},{3,2},{4,5},{5,4},{6,7},{7,6},{8,9},{9,8},{10,11... | collective-permute-start | bytes 49160 | tf_op jit(solution)/shard_map/ppermute | solution.py:541
  5.2 5.5 %collective-permute-start.5 = (f32[2,2048]{1,0:T(2,128)}, f32[2,2048]{1,0:T(2,128)S(1)}, u32[]{:S(2)}, u32[]{:S(2)}) collective-permute-start(f32[2,2048]{1,0:T(2,128)} %get-tuple-element.15.packet), channel_id=1, source_target_pairs={{0,2},{1,3},{2,0},{3,1},{4,6},{5,7},{6,4},{7,5},{8,10},{9,11},{10,... | collective-permute-start | bytes 49160 | tf_op jit(solution)/shard_map/ppermute | solution.py:541
  8.1 5.2 %collective-permute-start.6 = (f32[2,2048]{1,0:T(2,128)}, f32[2,2048]{1,0:T(2,128)S(1)}, u32[]{:S(2)}, u32[]{:S(2)}) collective-permute-start(f32[2,2048]{1,0:T(2,128)} %get-tuple-element.15.packet), channel_id=1, source_target_pairs={{0,3},{1,2},{2,1},{3,0},{4,7},{5,6},{6,5},{7,4},{8,11},{9,10},{10,... | collective-permute-start | bytes 49160 | tf_op jit(solution)/shard_map/ppermute | solution.py:541
  14.0 29.6 %copy-start = (f32[128,1024]{1,0:T(8,128)S(1)}, f32[128,1024]{1,0:T(8,128)}, u32[]{:S(2)}) copy-start(f32[128,1024]{1,0:T(8,128)} %visc.1) | copy-start | bytes 1572868
  14.1 5.8 %collective-permute-start.7 = (f32[4,2,2048]{2,1,0:T(2,128)S(1)}, f32[4,2,2048]{2,1,0:T(2,128)S(1)}, u32[]{:S(2)}, u32[]{:S(2)}) collective-permute-start(f32[4,2,2048]{2,1,0:T(2,128)S(1)} %pad_maximum_fusion.2.close), channel_id=1, source_target_pairs={{0,4},{4,0},{1,5},{5,1},{2,6},{6,2},{3,7},{7,3},{8,12},{12,8},{9,1... | collective-permute-start | bytes 196616 | tf_op jit(solution)/shard_map/ppermute | solution.py:543
  43.6 3.2 %collective-permute-start.12 = (f32[64,1024]{1,0:T(8,128)}, f32[64,1024]{1,0:T(8,128)S(1)}, u32[]{:S(2)}, u32[]{:S(2)}) collective-permute-start(f32[64,1024]{1,0:T(8,128)} %get-tuple-element.19), channel_id=1, source_target_pairs={{0,8},{8,0},{1,9},{9,1},{2,10},{10,2},{3,11},{11,3},{4,12},{12,4},... | collective-permute-start | bytes 786440 | tf_op jit(solution)/shard_map/ppermute | solution.py:556
  43.7 41.3 %collective-permute-start.21 = (f32[3,64,1024]{2,1,0:T(8,128)S(1)}, f32[3,64,1024]{2,1,0:T(8,128)S(1)}, u32[]{:S(2)}, u32[]{:S(2)}) collective-permute-start(f32[3,64,1024]{2,1,0:T(8,128)S(1)} %fusion.1), channel_id=1, source_target_pairs={{1,8},{2,9},{3,10},{4,11},{5,12},{6,13},{7,14},{8,1},{9,2},{10,3},... | collective-permute-start | bytes 2359304 | tf_op jit(solution)/shard_map/ppermute | solution.py:549
  46.9 12.5 %collective-permute-start.13 = (f32[32,1024]{1,0:T(8,128)S(1)}, f32[32,1024]{1,0:T(8,128)S(1)}, u32[]{:S(2)}, u32[]{:S(2)}) collective-permute-start(f32[32,1024]{1,0:T(8,128)S(1)} %get-tuple-element.22), channel_id=1, source_target_pairs={{0,16},{16,0},{1,17},{17,1},{2,18},{18,2},{3,19},{19,3},{4,20},{20... | collective-permute-start | bytes 393224 | tf_op jit(solution)/shard_map/ppermute | solution.py:562
  47.0 14.5 %collective-permute-start.16 = (f32[32,1024]{1,0:T(8,128)S(1)}, f32[32,1024]{1,0:T(8,128)S(1)}, u32[]{:S(2)}, u32[]{:S(2)}) collective-permute-start(f32[32,1024]{1,0:T(8,128)S(1)} %get-tuple-element.23), channel_id=1, source_target_pairs={{0,32},{32,0},{64,96},{96,64},{1,33},{33,1},{65,97},{97,65},{2,34}... | collective-permute-start | bytes 393224 | tf_op jit(solution)/shard_map/ppermute | solution.py:563
  59.4 5.1 %collective-permute-start.14 = (f32[32,1024]{1,0:T(8,128)S(1)}, f32[32,1024]{1,0:T(8,128)S(1)}, u32[]{:S(2)}, u32[]{:S(2)}) collective-permute-start(f32[32,1024]{1,0:T(8,128)S(1)} %add.41), channel_id=1, source_target_pairs={{0,32},{32,0},{64,96},{96,64},{1,33},{33,1},{65,97},{97,65},{2,34}... | collective-permute-start | bytes 393224 | tf_op jit(solution)/shard_map/ppermute | solution.py:564
  61.5 7.2 %collective-permute-start.17 = (f32[32,1024]{1,0:T(8,128)S(1)}, f32[32,1024]{1,0:T(8,128)S(1)}, u32[]{:S(2)}, u32[]{:S(2)}) collective-permute-start(f32[32,1024]{1,0:T(8,128)S(1)} %add.45), channel_id=1, source_target_pairs={{0,96},{32,64},{64,32},{96,0},{1,97},{33,65},{65,33},{97,1},{2,98}... | collective-permute-start | bytes 393224 | tf_op jit(solution)/shard_map/ppermute | solution.py:565
  64.5 7.2 %collective-permute-start.15 = (f32[32,1024]{1,0:T(8,128)S(1)}, f32[32,1024]{1,0:T(8,128)S(1)}, u32[]{:S(2)}, u32[]{:S(2)}) collective-permute-start(f32[32,1024]{1,0:T(8,128)S(1)} %add.42), channel_id=1, source_target_pairs={{0,96},{32,64},{64,32},{96,0},{1,97},{33,65},{65,33},{97,1},{2,98}... | collective-permute-start | bytes 393224 | tf_op jit(solution)/shard_map/ppermute | solution.py:568
  68.8 5.0 %collective-permute-start.18 = (f32[32,1024]{1,0:T(8,128)S(1)}, f32[32,1024]{1,0:T(8,128)S(1)}, u32[]{:S(2)}, u32[]{:S(2)}) collective-permute-start(f32[32,1024]{1,0:T(8,128)S(1)} %add.46), channel_id=1, source_target_pairs={{0,16},{16,0},{1,17},{17,1},{2,18},{18,2},{3,19},{19,3},{4,20},{20... | collective-permute-start | bytes 393224 | tf_op jit(solution)/shard_map/ppermute | solution.py:569
  73.9 11.7 %collective-permute-start.19 = (f32[64,1024]{1,0:T(8,128)S(1)}, f32[64,1024]{1,0:T(8,128)S(1)}, u32[]{:S(2)}, u32[]{:S(2)}) collective-permute-start(f32[64,1024]{1,0:T(8,128)S(1)} %pad_maximum_fusion.1.own), channel_id=1, source_target_pairs={{0,8},{8,0},{1,9},{9,1},{2,10},{10,2},{3,11},{11,3},{4,12},{12,4},... | collective-permute-start | bytes 786440 | tf_op jit(solution)/shard_map/ppermute | solution.py:571
  74.0 18.2 %collective-permute-start.20 = (f32[64,1024]{1,0:T(8,128)S(1)}, f32[64,1024]{1,0:T(8,128)S(1)}, u32[]{:S(2)}, u32[]{:S(2)}) collective-permute-start(f32[64,1024]{1,0:T(8,128)S(1)} %pad_maximum_fusion.1.own), channel_id=1, source_target_pairs={{1,8},{2,9},{3,10},{4,11},{5,12},{6,13},{7,14},{8,1},{9,2},{10,3},... | collective-permute-start | bytes 786440 | tf_op jit(solution)/shard_map/ppermute | solution.py:572
  77.5 5.5 %collective-permute-start.8 = (f32[4,1,2048]{2,1,0:T(1,128)S(1)}, f32[4,1,2048]{2,1,0:T(1,128)S(1)}, u32[]{:S(2)}, u32[]{:S(2)}) collective-permute-start(f32[4,1,2048]{2,1,0:T(1,128)S(1)} %copy-done.19), channel_id=1, source_target_pairs={{0,4},{4,0},{1,5},{5,1},{2,6},{6,2},{3,7},{7,3},{8,12},{12,8},{9,1... | collective-permute-start | bytes 98312 | tf_op jit(solution)/shard_map/ppermute | solution.py:557
  77.6 29.8 %collective-permute-start = (f32[16,128]{1,0:T(8,128)S(1)}, f32[16,128]{1,0:T(8,128)S(1)}, u32[]{:S(2)}, u32[]{:S(2)}) collective-permute-start(f32[16,128]{1,0:T(8,128)S(1)} %copy-done.21), channel_id=1, source_target_pairs={{0,8},{8,0},{1,9},{9,1},{2,10},{10,2},{3,11},{11,3},{4,12},{12,4},... | collective-permute-start | bytes 24584 | tf_op jit(solution)/shard_map/ppermute | solution.py:550
  83.0 24.4 %collective-permute-start.1 = (f32[16,128]{1,0:T(8,128)S(1)}, f32[16,128]{1,0:T(8,128)S(1)}, u32[]{:S(2)}, u32[]{:S(2)}) collective-permute-start(f32[16,128]{1,0:T(8,128)S(1)} %copy-done.20), channel_id=1, source_target_pairs={{8,16},{24,32},{40,48},{56,64},{72,80},{88,96},{104,112},{16,8},{3... | collective-permute-start | bytes 24584 | tf_op jit(solution)/shard_map/ppermute | solution.py:551
  85.0 18.9 %collective-permute-start.2 = (f32[16,64]{1,0:T(8,128)S(1)}, f32[16,64]{1,0:T(8,128)S(1)}, u32[]{:S(2)}, u32[]{:S(2)}) collective-permute-start(f32[16,64]{1,0:T(8,128)S(1)} %copy-done.23), channel_id=1, source_target_pairs={{0,1},{1,0},{2,3},{3,2},{4,5},{5,4},{6,7},{7,6},{8,9},{9,8},{10,11... | collective-permute-start | bytes 12296 | tf_op jit(solution)/shard_map/ppermute | solution.py:552
  85.6 19.1 %collective-permute-start.3 = (f32[16,64]{1,0:T(8,128)S(1)}, f32[16,64]{1,0:T(8,128)S(1)}, u32[]{:S(2)}, u32[]{:S(2)}) collective-permute-start(f32[16,64]{1,0:T(8,128)S(1)} %copy-done.22), channel_id=1, source_target_pairs={{1,2},{3,4},{5,6},{2,1},{4,3},{6,5},{9,10},{11,12},{13,14},{10,9},... | collective-permute-start | bytes 12296 | tf_op jit(solution)/shard_map/ppermute | solution.py:553
  103.3 11.2 %collective-permute-start.22 = (f32[64,1024]{1,0:T(8,128)}, f32[64,1024]{1,0:T(8,128)S(1)}, u32[]{:S(2)}, u32[]{:S(2)}) collective-permute-start(f32[64,1024]{1,0:T(8,128)} %solve.1), channel_id=1, source_target_pairs={{0,8},{8,0},{1,9},{9,1},{2,10},{10,2},{3,11},{11,3},{4,12},{12,4},... | collective-permute-start | bytes 786440 | tf_op jit(solution)/shard_map/ppermute | solution.py:574
  103.9 5.2 %collective-permute-start.10 = (f32[1,2048]{1,0:T(1,128)S(1)}, f32[1,2048]{1,0:T(1,128)S(1)}, u32[]{:S(2)}, u32[]{:S(2)}) collective-permute-start(f32[1,2048]{1,0:T(1,128)S(1)} %get-tuple-element.25), channel_id=1, source_target_pairs={{0,2},{1,3},{2,0},{3,1},{4,6},{5,7},{6,4},{7,5},{8,10},{9,11},{10,... | collective-permute-start | bytes 24584 | tf_op jit(solution)/shard_map/ppermute | solution.py:567
  104.7 4.9 %collective-permute-start.11 = (f32[1,2048]{1,0:T(1,128)S(1)}, f32[1,2048]{1,0:T(1,128)S(1)}, u32[]{:S(2)}, u32[]{:S(2)}) collective-permute-start(f32[1,2048]{1,0:T(1,128)S(1)} %get-tuple-element.24), channel_id=1, source_target_pairs={{0,3},{1,2},{2,1},{3,0},{4,7},{5,6},{6,5},{7,4},{8,11},{9,10},{10,... | collective-permute-start | bytes 24584 | tf_op jit(solution)/shard_map/ppermute | solution.py:567
  107.4 3.7 %collective-permute-start.9 = (f32[1,2048]{1,0:T(1,128)S(1)}, f32[1,2048]{1,0:T(1,128)S(1)}, u32[]{:S(2)}, u32[]{:S(2)}) collective-permute-start(f32[1,2048]{1,0:T(1,128)S(1)} %get-tuple-element.26), channel_id=1, source_target_pairs={{0,1},{1,0},{2,3},{3,2},{4,5},{5,4},{6,7},{7,6},{8,9},{9,8},{10,11... | collective-permute-start | bytes 24584 | tf_op jit(solution)/shard_map/ppermute | solution.py:567
  (23 other events, 235.8 us)
